TPU v7x, 32 devices: a whole 2x2x4 slice. The times are simulated.
32 devices in a mesh: pts: 8 (over z, x), help: 4 (over y, core).
Axes of the slice: x: 2, y: 2, z: 4, core: 2. Of those that a mesh axis runs over, the one named last changes fastest.
Arguments:
- src_points: bfloat16 [8192, 256], P(('pts', 'help')), may hold values from -8 to 8
- dst_points: bfloat16 [8192, 256], P(('pts', 'help')), may hold values from -8 to 8
- src_logw: float32 [8192], P(('pts', 'help')), may hold values from -1.2 to 1.2
- dst_logw: float32 [8192], P(('pts', 'help')), may hold values from -1.2 to 1.2
- init_g: float32 [8192], P(('pts', 'help')), may hold values from -2 to 7000
- pair_lists: int32 [32, 24], P(('pts', 'help')), may hold values from 0 to 31, as said below
- pair_counts: int32 [32], P(('pts', 'help')), may hold values from 3 to 24, as said below
Outputs:
- dual_f: float32 [8192], P(('pts', 'help'))
- dual_g: float32 [8192], P(('pts', 'help'))
Inputs may be any that keep to these rules, and one draw needn't show every extreme that they name: `pair_lists`: row block r's first pair_counts[r] entries are distinct, one of them is r itself, and each names a block whose points are held by an index of pts at most 3 away from the index that holds r; the later entries equal r. `pair_counts`: 24 is reached by some row block in every draw. The counts of the blocks held by one index of pts sum to at most 14 times the number of help devices; dealt out in turn to the help devices of that index, they give some device exactly 24 in every draw.
All inputs are finite; a program needn't handle non-finite values.
Results may differ from a plain program's by a relative error of at most 0.0003.
Values may be sent and summed in bfloat16 or wider, within the bound.
No kernel may reach another device: no remote copies, remote signals or barrier semaphores. Data moves between devices by JAX's collectives and lax.ppermute only.
A program may use at most 64 MiB of HBM per device.

v0:
```python
import jax
import jax.numpy as jnp
from jax import lax
from jax.sharding import PartitionSpec as P

PAIR_MOST = 24
REACH = 3
ITERS = 2


EPS = 0.25
NEGATIVE = -1e30


def shifted(block, axis, distance):
    devices = range(lax.axis_size(axis))
    route = [(i - distance, i) for i in devices if i - distance in devices]
    return lax.ppermute(block, axis, route)


def combined_all(part, axis, combine):
    gathered = jax.tree.map(lambda a: lax.all_gather(a, axis), part)

    def take(source):
        return jax.tree.map(lambda a: lax.dynamic_index_in_dim(a, source, 0, False), gathered)

    return lax.fori_loop(
        1, lax.axis_size(axis), lambda source, state: combine(state, take(source)), take(0)
    )


def merge_pair(earlier, later):
    peak = jnp.maximum(earlier[0], later[0])
    summed = earlier[1] * jnp.exp(earlier[0] - peak) + later[1] * jnp.exp(later[0] - peak)
    return (peak, summed)


def fold_into(tables, position, incoming):
    old_top = lax.dynamic_index_in_dim(tables[0], position, 0, keepdims=False)
    old_sum = lax.dynamic_index_in_dim(tables[1], position, 0, keepdims=False)
    new_top, new_sum = merge_pair((old_top, old_sum), incoming)
    return (
        lax.dynamic_update_index_in_dim(tables[0], new_top, position, 0),
        lax.dynamic_update_index_in_dim(tables[1], new_sum, position, 0),
    )


def pick_two(table, index_pair):
    return [
        lax.dynamic_index_in_dim(table, index_pair[member], 0, keepdims=False)
        for member in range(2)
    ]


def on_device(src_points, dst_points, src_logw, dst_logw, init_g, pair_lists, pair_counts):
    helpers = lax.axis_size("help")
    pts_total = lax.axis_size("pts")
    pts_here = lax.axis_index("pts")
    helper_here = lax.axis_index("help")
    block_rows = src_points.shape[0]
    spot_count = (2 * REACH + 1) * helpers
    offsets = list(range(-REACH, REACH + 1))
    far_offsets = [offset for offset in offsets if offset != 0]
    group_pts = lax.all_gather(dst_points, "help", axis=0, tiled=True)
    group_lw, group_g = (
        lax.all_gather(dst_logw, "help", axis=0, tiled=True),
        lax.all_gather(init_g, "help", axis=0, tiled=True),
    )
    nearby = {0: (group_pts, group_lw, group_g)}
    for heading in (1, -1):
        filled = 1
        while filled < REACH + 1:
            amount = min(filled, REACH + 1 - filled)
            picked = [nearby[-heading * member] for member in range(amount)]
            stacked_pts = jnp.stack([entry[0] for entry in picked])
            stacked_lw = jnp.stack([entry[1] for entry in picked])
            stacked_g = jnp.stack([entry[2] for entry in picked])
            arrived_pts = shifted(stacked_pts, "pts", heading * filled)
            arrived_vals = shifted((stacked_lw, stacked_g), "pts", heading * filled)
            for member in range(amount):
                nearby[-heading * (member + filled)] = (
                    arrived_pts[member],
                    arrived_vals[0][member],
                    arrived_vals[1][member],
                )
            filled += amount
    near_pts = jnp.concatenate([nearby[offset][0] for offset in offsets]).reshape(
        spot_count, block_rows, -1
    )
    near_lw = jnp.concatenate([nearby[offset][1] for offset in offsets]).reshape(
        spot_count, block_rows
    )
    potential = jnp.concatenate([nearby[offset][2] for offset in offsets]).reshape(
        spot_count, block_rows
    )
    near_half = 0.5 * jnp.sum(jnp.square(near_pts.astype(jnp.float32)), axis=2)
    row_pts = src_points[None]
    row_lw = src_logw[None]
    columns = pair_lists[0]
    active = jnp.arange(PAIR_MOST, dtype=jnp.int32) < pair_counts[0]
    row_slot = jnp.zeros((PAIR_MOST,), jnp.int32)
    spots = (columns // helpers - pts_here + REACH) * helpers + columns % helpers
    spots = jnp.clip(spots, 0, spot_count - 1)
    row_half = 0.5 * jnp.sum(jnp.square(row_pts.astype(jnp.float32)), axis=2)
    row_count = row_pts.shape[0]
    pair_total = columns.shape[0] // 2
    pair_spots = spots.reshape(pair_total, 2)
    pair_rows = row_slot.reshape(pair_total, 2)
    pair_active = active.reshape(pair_total, 2)

    def inner_tile(spot_pair, row_pair):
        lefts = pick_two(row_pts, row_pair)
        rights = pick_two(near_pts, spot_pair)
        return jnp.stack(
            [
                lax.dot_general(
                    lefts[member],
                    rights[member],
                    (((1,), (1,)), ((), ())),
                    preferred_element_type=jnp.float32,
                )
                for member in range(2)
            ]
        )

    def cost_of(inner_dot, spot_pair, row_pair):
        return (
            jnp.stack(pick_two(row_half, row_pair))[:, :, None]
            + jnp.stack(pick_two(near_half, spot_pair))[:, None, :]
            - inner_dot
        )

    source_pot = jnp.zeros((row_count, block_rows), jnp.float32)
    group_pot = jnp.zeros((helpers, block_rows), jnp.float32)
    for sweep_index in range(ITERS):
        target_pot = potential

        def row_step(carry, item):
            spot_pair, row_pair, active_pair = item
            inner_dot = inner_tile(spot_pair, row_pair)
            cost_tile = cost_of(inner_dot, spot_pair, row_pair)
            scores = (
                jnp.stack(pick_two(near_lw, spot_pair))[:, None, :]
                + (jnp.stack(pick_two(target_pot, spot_pair))[:, None, :] - cost_tile) / EPS
            )
            tile_top = jnp.max(scores, axis=2)
            tile_sum = jnp.sum(jnp.exp(scores - tile_top[:, :, None]), axis=2)
            tile_top = jnp.where(active_pair[:, None], tile_top, NEGATIVE)
            tile_sum = jnp.where(active_pair[:, None], tile_sum, 0.0)
            for member in range(2):
                carry = fold_into(carry, row_pair[member], (tile_top[member], tile_sum[member]))
            return (carry, None)

        row_initial = (
            jnp.full((row_count, block_rows), NEGATIVE, jnp.float32),
            jnp.zeros((row_count, block_rows), jnp.float32),
        )
        (row_top, row_sum), stored = lax.scan(
            row_step, row_initial, (pair_spots, pair_rows, pair_active)
        )
        source_pot = -EPS * (row_top + jnp.log(row_sum))

        def column_step(carry, item):
            spot_pair, row_pair, active_pair, kept = item
            inner_dot = inner_tile(spot_pair, row_pair)
            cost_tile = cost_of(inner_dot, spot_pair, row_pair)
            scores = (
                jnp.stack(pick_two(row_lw, row_pair))[:, :, None]
                + (jnp.stack(pick_two(source_pot, row_pair))[:, :, None] - cost_tile) / EPS
            )
            tile_top = jnp.max(scores, axis=1)
            tile_sum = jnp.sum(jnp.exp(scores - tile_top[:, None, :]), axis=1)
            tile_top = jnp.where(active_pair[:, None], tile_top, NEGATIVE)
            tile_sum = jnp.where(active_pair[:, None], tile_sum, 0.0)
            for member in range(2):
                carry = fold_into(carry, spot_pair[member], (tile_top[member], tile_sum[member]))
            return (carry, None)

        initial = (
            jnp.full((spot_count, block_rows), NEGATIVE, jnp.float32),
            jnp.zeros((spot_count, block_rows), jnp.float32),
        )
        result, unused = lax.scan(
            column_step, initial, (pair_spots, pair_rows, pair_active, stored)
        )
        col_top, col_sum = result
        slab_top = col_top.reshape(2 * REACH + 1, helpers, block_rows)
        slab_sum = col_sum.reshape(2 * REACH + 1, helpers, block_rows)
        gathered = (slab_top[REACH], slab_sum[REACH])
        for offset in far_offsets:
            arrived = shifted((slab_top[offset + REACH], slab_sum[offset + REACH]), "pts", offset)
            sender = pts_here - offset
            present = (sender >= 0) & (sender < pts_total)
            gathered = merge_pair(
                gathered,
                (jnp.where(present, arrived[0], NEGATIVE), jnp.where(present, arrived[1], 0.0)),
            )
        merged_top, merged_sum = combined_all((gathered[0], gathered[1]), "help", merge_pair)
        group_pot = -EPS * (merged_top + jnp.log(merged_sum))
        if sweep_index + 1 < ITERS:
            flat_pot = group_pot.reshape(-1)
            pieces = {0: flat_pot}
            for offset in far_offsets:
                pieces[offset] = shifted(flat_pot, "pts", -offset)
            potential = jnp.concatenate([pieces[offset] for offset in offsets]).reshape(
                spot_count, block_rows
            )
    own_f = source_pot[0]
    own_g = lax.dynamic_index_in_dim(group_pot, helper_here, 0, keepdims=False)
    return (own_f, own_g)


def solution(mesh):
    placed = (
        P(("pts", "help"), None),
        P(("pts", "help"), None),
        P(("pts", "help")),
        P(("pts", "help")),
        P(("pts", "help")),
        P(("pts", "help"), None),
        P(("pts", "help")),
    )
    return jax.shard_map(
        on_device,
        mesh=mesh,
        in_specs=placed,
        out_specs=(P(("pts", "help")), P(("pts", "help"))),
        check_vma=False,
    )
```

profile of v0, /device:TPU:0, one launch (start us, length us, event | category | flops | bytes accessed | tf_op | source)
XLA Modules:
  0.0 585.3 jit_solution(13396385603031042615)
XLA Ops:
  0.7 8.9 %all_gather.35 = bf16[1024,256]{1,0:T(8,128)(2,1)S(1)} all-gather(bf16[256,256]{1,0:T(8,128)(2,1)} %param.20), channel_id=1, replica_groups=mesh['pts'=8,'help'=4] {'help'}, dimensions={0}, use_global_device_ids=true | all-gather | bytes 655360 | tf_op jit(solution)/shard_map/all_gather | solution.py:64
  10.8 4.6 collective-permute-start.8
  15.4 5.3 all-gather.4
  20.7 4.3 collective-permute-start
  26.3 5.3 all-gather.5
  31.5 4.5 collective-permute-start.4
  39.6 6.5 %collective-permute-start.9 = (bf16[2,1024,256]{2,1,0:T(8,128)(2,1)}, bf16[2,1024,256]{2,1,0:T(8,128)(2,1)}, u32[]{:S(2)}, u32[]{:S(2)}) collective-permute-start(bf16[2,1024,256]{2,1,0:T(8,128)(2,1)} %get-tuple-element.1173), channel_id=1, source_target_pairs={{0,8},{4,12},{8,16},{12,20},{16,24},{20,28},{1,9},{5,13},{9,17},{1... | collective-permute-start | bytes 3145736 | tf_op jit(solution)/shard_map/ppermute | solution.py:18
  53.8 4.5 collective-permute-start.5
  60.8 7.1 %collective-permute-done.1 = f32[2,1024]{1,0:T(2,128)S(1)} collective-permute-done((f32[2,1024]{1,0:T(2,128)S(1)}, f32[2,1024]{1,0:T(2,128)S(1)}, u32[]{:S(2)}, u32[]{:S(2)}) %collective-permute-start.1) | collective-permute-done | bytes 8224 | tf_op jit(solution)/shard_map/ppermute | solution.py:18
  71.9 23.1 %collective-permute-done.11 = bf16[2,1024,256]{2,1,0:T(8,128)(2,1)S(1)} collective-permute-done((bf16[2,1024,256]{2,1,0:T(8,128)(2,1)S(1)}, bf16[2,1024,256]{2,1,0:T(8,128)(2,1)S(1)}, u32[]{:S(2)}, u32[]{:S(2)}) %collective-permute-start.11) | collective-permute-done | bytes 1048608 | tf_op jit(solution)/shard_map/ppermute | solution.py:18
  97.9 89.1 %while.96 = (s32[]{:T(128)}, f32[1,256]{1,0:T(1,128)S(1)}, f32[1,256]{1,0:T(1,128)S(1)}, pred[12,2]{1,0:T(8,128)(4,1)S(1)}, s32[12,2]{0,1:T(2,128)S(1)}, /*index...) while((s32[]{:T(128)}, f32[1,256]{1,0:T(1,128)S(1)}, ...), condition=%wide.region_5.6_spmd.clone, body=%wide.region_2.5_spmd.clone.sunk | while | flops 69080064 | bytes 2160921 | solution.py:158
  187.1 92.2 %while.92 = (s32[]{:T(128)}, f32[28,256]{1,0:T(8,128)S(1)}, f32[28,256]{1,0:T(8,128)S(1)}, s32[12,2]{0,1:T(2,128)S(1)}, pred[12,2]{1,0:T(8,128)(4,1)S(1)}, /*ind...) while((s32[]{:T(128)}, f32[28,256]{1,0:T(8,128)S(1)}, ...), condition=%wide.region_9.10_spmd, body=%wide.region_6.9_spmd.sunk | while | flops 69078536 | bytes 2156831 | solution.py:183
  283.3 4.5 collective-permute-start.15
  287.8 4.6 collective-permute-start.16
  292.5 6.3 %collective-permute-start.17 = (f32[4,256]{1,0:T(4,128)S(1)}, f32[4,256]{1,0:T(4,128)S(1)}, u32[]{:S(2)}, u32[]{:S(2)}) collective-permute-start(f32[4,256]{1,0:T(4,128)S(1)} %get-tuple-element.1193), channel_id=1, source_target_pairs={{0,12},{4,16},{8,20},{12,24},{16,28},{1,13},{5,17},{9,21},{13,25},... | collective-permute-start | bytes 12296 | tf_op jit(solution)/shard_map/ppermute | solution.py:18
  302.7 4.5 collective-permute-start.21
  307.3 4.6 collective-permute-start.22
  311.9 6.3 %collective-permute-start.23 = (f32[4,256]{1,0:T(4,128)S(1)}, f32[4,256]{1,0:T(4,128)S(1)}, u32[]{:S(2)}, u32[]{:S(2)}) collective-permute-start(f32[4,256]{1,0:T(4,128)S(1)} %get-tuple-element.1187), channel_id=1, source_target_pairs={{0,12},{4,16},{8,20},{12,24},{16,28},{1,13},{5,17},{9,21},{13,25},... | collective-permute-start | bytes 12296 | tf_op jit(solution)/shard_map/ppermute | solution.py:18
  319.5 5.2 all-gather.7
  324.8 5.2 all-gather.6
  330.1 5.1 collective-permute-start.24
  337.1 3.4 collective-permute-start.26
  351.4 89.6 %while.97 = (s32[]{:T(128)}, f32[1,256]{1,0:T(1,128)S(1)}, f32[1,256]{1,0:T(1,128)S(1)}, pred[12,2]{1,0:T(8,128)(4,1)S(1)}, s32[12,2]{0,1:T(2,128)S(1)}, /*index...) while((s32[]{:T(128)}, f32[1,256]{1,0:T(1,128)S(1)}, ...), condition=%wide.region_15.16_spmd.clone, body=%wide.region_12.15_spmd.clone.sunk | while | flops 69080064 | bytes 2160921 | solution.py:158
  441.6 91.5 %while.94 = (s32[]{:T(128)}, f32[28,256]{1,0:T(8,128)S(1)}, f32[28,256]{1,0:T(8,128)S(1)}, s32[12,2]{0,1:T(2,128)S(1)}, pred[12,2]{1,0:T(8,128)(4,1)S(1)}, /*ind...) while((s32[]{:T(128)}, f32[28,256]{1,0:T(8,128)S(1)}, ...), condition=%wide.region_19.20_spmd, body=%wide.region_16.19_spmd.sunk | while | flops 69078536 | bytes 2156831 | solution.py:183
  537.0 4.5 collective-permute-start.33
  541.6 5.5 collective-permute-start.34
  547.2 6.3 %collective-permute-start.35 = (f32[4,256]{1,0:T(4,128)S(1)}, f32[4,256]{1,0:T(4,128)S(1)}, u32[]{:S(2)}, u32[]{:S(2)}) collective-permute-start(f32[4,256]{1,0:T(4,128)S(1)} %get-tuple-element.1181), channel_id=1, source_target_pairs={{0,12},{4,16},{8,20},{12,24},{16,28},{1,13},{5,17},{9,21},{13,25},... | collective-permute-start | bytes 12296 | tf_op jit(solution)/shard_map/ppermute | solution.py:18
  557.4 4.5 collective-permute-start.39
  561.9 4.6 collective-permute-start.40
  566.6 6.3 %collective-permute-start.41 = (f32[4,256]{1,0:T(4,128)S(1)}, f32[4,256]{1,0:T(4,128)S(1)}, u32[]{:S(2)}, u32[]{:S(2)}) collective-permute-start(f32[4,256]{1,0:T(4,128)S(1)} %get-tuple-element.1175), channel_id=1, source_target_pairs={{0,12},{4,16},{8,20},{12,24},{16,28},{1,13},{5,17},{9,21},{13,25},... | collective-permute-start | bytes 12296 | tf_op jit(solution)/shard_map/ppermute | solution.py:18
  574.2 5.2 all-gather.9
  579.4 5.2 all-gather.8
  (881 shorter events, 231.9 us)
Async XLA Ops:
  9.5 27.6 %collective-permute-start.10 = (bf16[1,1024,256]{2,1,0:T(8,128)(2,1)S(1)}, bf16[1,1024,256]{2,1,0:T(8,128)(2,1)S(1)}, u32[]{:S(2)}, u32[]{:S(2)}) collective-permute-start(bf16[1,1024,256]{2,1,0:T(8,128)(2,1)S(1)} %bitcast.251), channel_id=1, source_target_pairs={{4,0},{8,4},{12,8},{16,12},{20,16},{24,20},{28,24},{5,1},{9,5},{13... | collective-permute-start | bytes 1572872 | tf_op jit(solution)/shard_map/ppermute | solution.py:18
  10.8 27.6 %collective-permute-start.8 = (bf16[1,1024,256]{2,1,0:T(8,128)(2,1)S(1)}, bf16[1,1024,256]{2,1,0:T(8,128)(2,1)S(1)}, u32[]{:S(2)}, u32[]{:S(2)}) collective-permute-start(bf16[1,1024,256]{2,1,0:T(8,128)(2,1)S(1)} %bitcast.252), channel_id=1, source_target_pairs={{0,4},{4,8},{8,12},{12,16},{16,20},{20,24},{24,28},{1,5},{5,9},{9,... | collective-permute-start | bytes 1572872 | tf_op jit(solution)/shard_map/ppermute | solution.py:18
  20.7 27.5 %collective-permute-start = (f32[1,1024]{1,0:T(1,128)S(1)}, f32[1,1024]{1,0:T(1,128)S(1)}, u32[]{:S(2)}, u32[]{:S(2)}) collective-permute-start(f32[1,1024]{1,0:T(1,128)S(1)} %bitcast.257), channel_id=1, source_target_pairs={{0,4},{4,8},{8,12},{12,16},{16,20},{20,24},{24,28},{1,5},{5,9},{9,... | collective-permute-start | bytes 12296 | tf_op jit(solution)/shard_map/ppermute | solution.py:18
  25.0 23.3 %collective-permute-start.2 = (f32[1,1024]{1,0:T(1,128)S(1)}, f32[1,1024]{1,0:T(1,128)S(1)}, u32[]{:S(2)}, u32[]{:S(2)}) collective-permute-start(f32[1,1024]{1,0:T(1,128)S(1)} %bitcast.258), channel_id=1, source_target_pairs={{4,0},{8,4},{12,8},{16,12},{20,16},{24,20},{28,24},{5,1},{9,5},{13... | collective-permute-start | bytes 12296 | tf_op jit(solution)/shard_map/ppermute | solution.py:18
  31.5 20.5 %collective-permute-start.4 = (f32[1,1024]{1,0:T(1,128)S(1)}, f32[1,1024]{1,0:T(1,128)S(1)}, u32[]{:S(2)}, u32[]{:S(2)}) collective-permute-start(f32[1,1024]{1,0:T(1,128)S(1)} %bitcast.254), channel_id=1, source_target_pairs={{0,4},{4,8},{8,12},{12,16},{16,20},{20,24},{24,28},{1,5},{5,9},{9,... | collective-permute-start | bytes 12296 | tf_op jit(solution)/shard_map/ppermute | solution.py:18
  37.1 15.0 %collective-permute-start.6 = (f32[1,1024]{1,0:T(1,128)S(1)}, f32[1,1024]{1,0:T(1,128)S(1)}, u32[]{:S(2)}, u32[]{:S(2)}) collective-permute-start(f32[1,1024]{1,0:T(1,128)S(1)} %bitcast.255), channel_id=1, source_target_pairs={{4,0},{8,4},{12,8},{16,12},{20,16},{24,20},{28,24},{5,1},{9,5},{13... | collective-permute-start | bytes 12296 | tf_op jit(solution)/shard_map/ppermute | solution.py:18
  39.6 30.0 %collective-permute-start.9 = (bf16[2,1024,256]{2,1,0:T(8,128)(2,1)}, bf16[2,1024,256]{2,1,0:T(8,128)(2,1)}, u32[]{:S(2)}, u32[]{:S(2)}) collective-permute-start(bf16[2,1024,256]{2,1,0:T(8,128)(2,1)} %get-tuple-element.1173), channel_id=1, source_target_pairs={{0,8},{4,12},{8,16},{12,20},{16,24},{20,28},{1,9},{5,13},{9,17},{1... | collective-permute-start | bytes 3145736 | tf_op jit(solution)/shard_map/ppermute | solution.py:18
  48.3 19.7 %collective-permute-start.1 = (f32[2,1024]{1,0:T(2,128)S(1)}, f32[2,1024]{1,0:T(2,128)S(1)}, u32[]{:S(2)}, u32[]{:S(2)}) collective-permute-start(f32[2,1024]{1,0:T(2,128)S(1)} %get-tuple-element.1201), channel_id=1, source_target_pairs={{0,8},{4,12},{8,16},{12,20},{16,24},{20,28},{1,9},{5,13},{9,17},{1... | collective-permute-start | bytes 24584 | tf_op jit(solution)/shard_map/ppermute | solution.py:18
  50.8 17.2 %collective-permute-start.3 = (f32[2,1024]{1,0:T(2,128)S(1)}, f32[2,1024]{1,0:T(2,128)S(1)}, u32[]{:S(2)}, u32[]{:S(2)}) collective-permute-start(f32[2,1024]{1,0:T(2,128)S(1)} %get-tuple-element.1200), channel_id=1, source_target_pairs={{8,0},{12,4},{16,8},{20,12},{24,16},{28,20},{9,1},{13,5},{17,9},{2... | collective-permute-start | bytes 24584 | tf_op jit(solution)/shard_map/ppermute | solution.py:18
  53.8 14.2 %collective-permute-start.5 = (f32[2,1024]{1,0:T(2,128)S(1)}, f32[2,1024]{1,0:T(2,128)S(1)}, u32[]{:S(2)}, u32[]{:S(2)}) collective-permute-start(f32[2,1024]{1,0:T(2,128)S(1)} %get-tuple-element.1199), channel_id=1, source_target_pairs={{0,8},{4,12},{8,16},{12,20},{16,24},{20,28},{1,9},{5,13},{9,17},{1... | collective-permute-start | bytes 24584 | tf_op jit(solution)/shard_map/ppermute | solution.py:18
  68.3 26.7 %collective-permute-start.11 = (bf16[2,1024,256]{2,1,0:T(8,128)(2,1)S(1)}, bf16[2,1024,256]{2,1,0:T(8,128)(2,1)S(1)}, u32[]{:S(2)}, u32[]{:S(2)}) collective-permute-start(bf16[2,1024,256]{2,1,0:T(8,128)(2,1)S(1)} %get-tuple-element.1172), channel_id=1, source_target_pairs={{8,0},{12,4},{16,8},{20,12},{24,16},{28,20},{9,1},{13,5},{17,9},{2... | collective-permute-start | bytes 3145736 | tf_op jit(solution)/shard_map/ppermute | solution.py:18
  279.4 13.1 %collective-permute-start.12 = (f32[4,256]{1,0:T(4,128)S(1)}, f32[4,256]{1,0:T(4,128)S(1)}, u32[]{:S(2)}, u32[]{:S(2)}) collective-permute-start(f32[4,256]{1,0:T(4,128)S(1)} %get-tuple-element.1192), channel_id=1, source_target_pairs={{12,0},{16,4},{20,8},{24,12},{28,16},{13,1},{17,5},{21,9},{25,13},... | collective-permute-start | bytes 12296 | tf_op jit(solution)/shard_map/ppermute | solution.py:18
  280.7 18.1 %collective-permute-start.13 = (f32[4,256]{1,0:T(4,128)S(1)}, f32[4,256]{1,0:T(4,128)S(1)}, u32[]{:S(2)}, u32[]{:S(2)}) collective-permute-start(f32[4,256]{1,0:T(4,128)S(1)} %get-tuple-element.1197), channel_id=1, source_target_pairs={{8,0},{12,4},{16,8},{20,12},{24,16},{28,20},{9,1},{13,5},{17,9},{2... | collective-permute-start | bytes 12296 | tf_op jit(solution)/shard_map/ppermute | solution.py:18
  282.0 18.1 %collective-permute-start.14 = (f32[4,256]{1,0:T(4,128)S(1)}, f32[4,256]{1,0:T(4,128)S(1)}, u32[]{:S(2)}, u32[]{:S(2)}) collective-permute-start(f32[4,256]{1,0:T(4,128)S(1)} %get-tuple-element.1196), channel_id=1, source_target_pairs={{4,0},{8,4},{12,8},{16,12},{20,16},{24,20},{28,24},{5,1},{9,5},{13... | collective-permute-start | bytes 12296 | tf_op jit(solution)/shard_map/ppermute | solution.py:18
  283.3 18.1 %collective-permute-start.15 = (f32[4,256]{1,0:T(4,128)S(1)}, f32[4,256]{1,0:T(4,128)S(1)}, u32[]{:S(2)}, u32[]{:S(2)}) collective-permute-start(f32[4,256]{1,0:T(4,128)S(1)} %get-tuple-element.1195), channel_id=1, source_target_pairs={{0,4},{4,8},{8,12},{12,16},{16,20},{20,24},{24,28},{1,5},{5,9},{9,... | collective-permute-start | bytes 12296 | tf_op jit(solution)/shard_map/ppermute | solution.py:18
  287.8 14.9 %collective-permute-start.16 = (f32[4,256]{1,0:T(4,128)S(1)}, f32[4,256]{1,0:T(4,128)S(1)}, u32[]{:S(2)}, u32[]{:S(2)}) collective-permute-start(f32[4,256]{1,0:T(4,128)S(1)} %get-tuple-element.1194), channel_id=1, source_target_pairs={{0,8},{4,12},{8,16},{12,20},{16,24},{20,28},{1,9},{5,13},{9,17},{1... | collective-permute-start | bytes 12296 | tf_op jit(solution)/shard_map/ppermute | solution.py:18
  292.5 14.8 %collective-permute-start.17 = (f32[4,256]{1,0:T(4,128)S(1)}, f32[4,256]{1,0:T(4,128)S(1)}, u32[]{:S(2)}, u32[]{:S(2)}) collective-permute-start(f32[4,256]{1,0:T(4,128)S(1)} %get-tuple-element.1193), channel_id=1, source_target_pairs={{0,12},{4,16},{8,20},{12,24},{16,28},{1,13},{5,17},{9,21},{13,25},... | collective-permute-start | bytes 12296 | tf_op jit(solution)/shard_map/ppermute | solution.py:18
  298.8 13.1 %collective-permute-start.18 = (f32[4,256]{1,0:T(4,128)S(1)}, f32[4,256]{1,0:T(4,128)S(1)}, u32[]{:S(2)}, u32[]{:S(2)}) collective-permute-start(f32[4,256]{1,0:T(4,128)S(1)} %get-tuple-element.1186), channel_id=1, source_target_pairs={{12,0},{16,4},{20,8},{24,12},{28,16},{13,1},{17,5},{21,9},{25,13},... | collective-permute-start | bytes 12296 | tf_op jit(solution)/shard_map/ppermute | solution.py:18
  300.1 18.1 %collective-permute-start.19 = (f32[4,256]{1,0:T(4,128)S(1)}, f32[4,256]{1,0:T(4,128)S(1)}, u32[]{:S(2)}, u32[]{:S(2)}) collective-permute-start(f32[4,256]{1,0:T(4,128)S(1)} %get-tuple-element.1191), channel_id=1, source_target_pairs={{8,0},{12,4},{16,8},{20,12},{24,16},{28,20},{9,1},{13,5},{17,9},{2... | collective-permute-start | bytes 12296 | tf_op jit(solution)/shard_map/ppermute | solution.py:18
  301.4 16.8 %collective-permute-start.20 = (f32[4,256]{1,0:T(4,128)S(1)}, f32[4,256]{1,0:T(4,128)S(1)}, u32[]{:S(2)}, u32[]{:S(2)}) collective-permute-start(f32[4,256]{1,0:T(4,128)S(1)} %get-tuple-element.1190), channel_id=1, source_target_pairs={{4,0},{8,4},{12,8},{16,12},{20,16},{24,20},{28,24},{5,1},{9,5},{13... | collective-permute-start | bytes 12296 | tf_op jit(solution)/shard_map/ppermute | solution.py:18
  302.7 15.5 %collective-permute-start.21 = (f32[4,256]{1,0:T(4,128)S(1)}, f32[4,256]{1,0:T(4,128)S(1)}, u32[]{:S(2)}, u32[]{:S(2)}) collective-permute-start(f32[4,256]{1,0:T(4,128)S(1)} %get-tuple-element.1189), channel_id=1, source_target_pairs={{0,4},{4,8},{8,12},{12,16},{16,20},{20,24},{24,28},{1,5},{5,9},{9,... | collective-permute-start | bytes 12296 | tf_op jit(solution)/shard_map/ppermute | solution.py:18
  330.1 13.0 %collective-permute-start.24 = (f32[1024]{0:T(1024)S(1)}, f32[1024]{0:T(1024)S(1)}, u32[]{:S(2)}, u32[]{:S(2)}) collective-permute-start(f32[1024]{0:T(1024)S(1)} %bitcast.265), channel_id=1, source_target_pairs={{0,12},{4,16},{8,20},{12,24},{16,28},{1,13},{5,17},{9,21},{13,25},... | collective-permute-start | bytes 12296 | tf_op jit(solution)/shard_map/ppermute | solution.py:18
  533.1 14.0 %collective-permute-start.30 = (f32[4,256]{1,0:T(4,128)S(1)}, f32[4,256]{1,0:T(4,128)S(1)}, u32[]{:S(2)}, u32[]{:S(2)}) collective-permute-start(f32[4,256]{1,0:T(4,128)S(1)} %get-tuple-element.1180), channel_id=1, source_target_pairs={{12,0},{16,4},{20,8},{24,12},{28,16},{13,1},{17,5},{21,9},{25,13},... | collective-permute-start | bytes 12296 | tf_op jit(solution)/shard_map/ppermute | solution.py:18
  534.4 19.0 %collective-permute-start.31 = (f32[4,256]{1,0:T(4,128)S(1)}, f32[4,256]{1,0:T(4,128)S(1)}, u32[]{:S(2)}, u32[]{:S(2)}) collective-permute-start(f32[4,256]{1,0:T(4,128)S(1)} %get-tuple-element.1185), channel_id=1, source_target_pairs={{8,0},{12,4},{16,8},{20,12},{24,16},{28,20},{9,1},{13,5},{17,9},{2... | collective-permute-start | bytes 12296 | tf_op jit(solution)/shard_map/ppermute | solution.py:18
  535.7 19.0 %collective-permute-start.32 = (f32[4,256]{1,0:T(4,128)S(1)}, f32[4,256]{1,0:T(4,128)S(1)}, u32[]{:S(2)}, u32[]{:S(2)}) collective-permute-start(f32[4,256]{1,0:T(4,128)S(1)} %get-tuple-element.1184), channel_id=1, source_target_pairs={{4,0},{8,4},{12,8},{16,12},{20,16},{24,20},{28,24},{5,1},{9,5},{13... | collective-permute-start | bytes 12296 | tf_op jit(solution)/shard_map/ppermute | solution.py:18
  537.0 19.0 %collective-permute-start.33 = (f32[4,256]{1,0:T(4,128)S(1)}, f32[4,256]{1,0:T(4,128)S(1)}, u32[]{:S(2)}, u32[]{:S(2)}) collective-permute-start(f32[4,256]{1,0:T(4,128)S(1)} %get-tuple-element.1183), channel_id=1, source_target_pairs={{0,4},{4,8},{8,12},{12,16},{16,20},{20,24},{24,28},{1,5},{5,9},{9,... | collective-permute-start | bytes 12296 | tf_op jit(solution)/shard_map/ppermute | solution.py:18
  541.6 15.8 %collective-permute-start.34 = (f32[4,256]{1,0:T(4,128)S(1)}, f32[4,256]{1,0:T(4,128)S(1)}, u32[]{:S(2)}, u32[]{:S(2)}) collective-permute-start(f32[4,256]{1,0:T(4,128)S(1)} %get-tuple-element.1182), channel_id=1, source_target_pairs={{0,8},{4,12},{8,16},{12,20},{16,24},{20,28},{1,9},{5,13},{9,17},{1... | collective-permute-start | bytes 12296 | tf_op jit(solution)/shard_map/ppermute | solution.py:18
  547.2 14.8 %collective-permute-start.35 = (f32[4,256]{1,0:T(4,128)S(1)}, f32[4,256]{1,0:T(4,128)S(1)}, u32[]{:S(2)}, u32[]{:S(2)}) collective-permute-start(f32[4,256]{1,0:T(4,128)S(1)} %get-tuple-element.1181), channel_id=1, source_target_pairs={{0,12},{4,16},{8,20},{12,24},{16,28},{1,13},{5,17},{9,21},{13,25},... | collective-permute-start | bytes 12296 | tf_op jit(solution)/shard_map/ppermute | solution.py:18
  553.4 13.1 %collective-permute-start.36 = (f32[4,256]{1,0:T(4,128)S(1)}, f32[4,256]{1,0:T(4,128)S(1)}, u32[]{:S(2)}, u32[]{:S(2)}) collective-permute-start(f32[4,256]{1,0:T(4,128)S(1)} %get-tuple-element.1174), channel_id=1, source_target_pairs={{12,0},{16,4},{20,8},{24,12},{28,16},{13,1},{17,5},{21,9},{25,13},... | collective-permute-start | bytes 12296 | tf_op jit(solution)/shard_map/ppermute | solution.py:18
  554.8 18.1 %collective-permute-start.37 = (f32[4,256]{1,0:T(4,128)S(1)}, f32[4,256]{1,0:T(4,128)S(1)}, u32[]{:S(2)}, u32[]{:S(2)}) collective-permute-start(f32[4,256]{1,0:T(4,128)S(1)} %get-tuple-element.1179), channel_id=1, source_target_pairs={{8,0},{12,4},{16,8},{20,12},{24,16},{28,20},{9,1},{13,5},{17,9},{2... | collective-permute-start | bytes 12296 | tf_op jit(solution)/shard_map/ppermute | solution.py:18
  556.1 16.8 %collective-permute-start.38 = (f32[4,256]{1,0:T(4,128)S(1)}, f32[4,256]{1,0:T(4,128)S(1)}, u32[]{:S(2)}, u32[]{:S(2)}) collective-permute-start(f32[4,256]{1,0:T(4,128)S(1)} %get-tuple-element.1178), channel_id=1, source_target_pairs={{4,0},{8,4},{12,8},{16,12},{20,16},{24,20},{28,24},{5,1},{9,5},{13... | collective-permute-start | bytes 12296 | tf_op jit(solution)/shard_map/ppermute | solution.py:18
  557.4 15.5 %collective-permute-start.39 = (f32[4,256]{1,0:T(4,128)S(1)}, f32[4,256]{1,0:T(4,128)S(1)}, u32[]{:S(2)}, u32[]{:S(2)}) collective-permute-start(f32[4,256]{1,0:T(4,128)S(1)} %get-tuple-element.1177), channel_id=1, source_target_pairs={{0,4},{4,8},{8,12},{12,16},{16,20},{20,24},{24,28},{1,5},{5,9},{9,... | collective-permute-start | bytes 12296 | tf_op jit(solution)/shard_map/ppermute | solution.py:18
  (15 other events, 205.1 us)
where the time goes:
time: 591 us; the launch traced here: 585 us
  loops' own time  185 us (31%)
  starting transfers between devices  127 us (21%)
  matrix products  108 us (18%)
  local copies, waits for them, and re-layouts  42 us (7%)
  other arithmetic  40.9 us (7%)
  blocking collectives  40.3 us (7%)
  waiting for transfers between devices  39.6 us (7%)
    ppermute x42, starting transfers between devices, shifted(): return lax.ppermute(block, axis, route)  127 us
    dot_general x96, matrix products, inner_tile(): lax.dot_general(lefts[member], rights[member], (((1,), (1,)), ((), ())),...  108 us
    another operation x2, loops' own time, on_device(): lax.scan(column_step, initial, (pair_spots, pair_rows, pair_active, stored))  93.4 us
    another operation x2, loops' own time, on_device(): lax.scan(row_step, row_initial, (pair_spots, pair_rows, pair_active))  91.8 us
    ppermute x42, waiting for transfers between devices, shifted(): return lax.ppermute(block, axis, route)  39.6 us
    slice x48, local copies, waits for them, and re-layouts, pick_two(): index_pair[member]  26.4 us
    all_gather x4, blocking collectives, combined_all(): gathered = jax.tree.map(lambda a: lax.all_gather(a, axis), part)  20.8 us
  transfers between devices with their start and end apart: 42, of which 7 were waited for; matrix products, arithmetic and copies ran while one was open for 2% of the time, Pallas kernels for 0%

commit v1 on v0

v1 whole, which is shorter than its diff:
```python
import functools
import math

import jax
import jax.numpy as jnp
from jax import lax
from jax.experimental import pallas as pl
from jax.experimental.pallas import tpu as pltpu
from jax.sharding import PartitionSpec as P

REACH = 3
SPOTS = 2 * REACH + 1
EPS = 0.25
NEGATIVE = -1e30
LOG2E = math.log2(math.e)
SCALE = LOG2E / EPS
BACK = EPS / LOG2E
TAIL = 16
LANES = 128
CHUNK = 16

f32 = jnp.float32
bf16 = jnp.bfloat16


def pieces(value):
    high = value.astype(bf16).astype(f32)
    rest = value - high
    middle = rest.astype(bf16).astype(f32)
    low = (rest - middle).astype(bf16).astype(f32)
    return [high, middle, low]


def stacked(rows, width):
    index = lax.broadcasted_iota(jnp.int32, (TAIL, width), 0)
    out = jnp.zeros((TAIL, width), f32)
    for at, row in enumerate(rows):
        out = jnp.where(index == at, row, out)
    return out.astype(bf16)


def half_norms(points):
    wide = points.astype(f32)
    square = wide * wide
    high = square.astype(bf16)
    low = (square - high.astype(f32)).astype(bf16)
    ones = jnp.ones((8, points.shape[1]), bf16)
    dims = (((1,), (1,)), ((), ()))
    total = lax.dot_general(ones, high, dims, preferred_element_type=f32) + lax.dot_general(
        ones, low, dims, preferred_element_type=f32
    )
    return 0.5 * total[0:1]


def log_sum(top, values):
    return top + jnp.log(values) * LOG2E


def merged(parts):
    top = functools.reduce(jnp.maximum, parts)
    return log_sum(top, sum(jnp.exp2(part - top) for part in parts))


def prepare(base, lists, counts, src, dst, src_lw, dst_lw, start, src_pay, dst_pay, halves):
    block = src.shape[0]
    width = src.shape[1]
    src_half = half_norms(src[...])
    dst_half = half_norms(dst[...])
    halves[0:1, :] = src_half
    halves[1:2, :] = dst_half
    lane = lax.broadcasted_iota(jnp.int32, (1, width), 1) + base[0]
    count = counts[0]
    paired = jnp.zeros((1, width), f32)
    for entry in range(lists.shape[1]):
        column = jnp.where(entry < count, lists[0, entry], lists[0, 0])
        paired = jnp.where(lane == column, 1.0, paired)
    src_pay[0:block, :] = src[...]
    src_pay[block:, :] = stacked(pieces(src_lw[...] * LOG2E) + [paired], width)
    dst_pay[0:block, :] = dst[...]
    weight = dst_lw[...] * LOG2E
    first = weight + (start[...] - dst_half) * SCALE
    dst_pay[block:, :] = stacked(pieces(first) + pieces(weight), width)


def sweep(rows_ref, cols_ref, value_of, bias_ref, dots, tops, sums, bias_row, emit):
    row_blocks = rows_ref.shape[0]
    col_blocks = cols_ref.shape[0]
    block = tops.shape[0]

    def one(at, carry):
        for k in range(col_blocks):
            dots[:, k * block : (k + 1) * block] = lax.dot_general(
                rows_ref[at, 0:block, :],
                cols_ref[k, 0:block, :],
                (((1,), (1,)), ((), ())),
                preferred_element_type=f32,
            )
            bias_row[:, k * block : (k + 1) * block] = (
                value_of(k) + bias_ref[pl.ds(at, 1), k * block : (k + 1) * block]
            )

        def chunk(step, inner):
            start = pl.multiple_of(step * CHUNK, CHUNK)
            parts = [
                dots[pl.ds(start, CHUNK), lane : lane + LANES] * SCALE
                + bias_row[:, lane : lane + LANES]
                for lane in range(0, col_blocks * block, LANES)
            ]
            top = functools.reduce(jnp.maximum, parts)
            tops[pl.ds(start, CHUNK), :] = top
            sums[pl.ds(start, CHUNK), :] = sum(jnp.exp2(part - top) for part in parts)
            return inner

        lax.fori_loop(0, block // CHUNK, chunk, 0)
        turned = tops[...].T
        peak = jnp.max(turned, axis=0, keepdims=True)
        total = jnp.sum(sums[...].T * jnp.exp2(turned - peak), axis=0, keepdims=True)
        emit(at, log_sum(peak, total))
        return carry

    lax.fori_loop(0, row_blocks, one, 0)


def first_rows(here, src_pay, dst_pay, out, row_bias, col_bias, src_value, dst_value, dots, tops, sums, line, value):
    helpers = src_pay.shape[0]
    block = tops.shape[0]
    lane = lax.broadcasted_iota(jnp.int32, (1, src_pay.shape[2]), 1)
    for spot in range(SPOTS):
        tail = dst_pay[spot, block:, :].astype(f32)
        value[spot : spot + 1, :] = tail[0:1] + tail[1:2] + tail[2:3]
        dst_value[spot : spot + 1, :] = tail[3:4] + tail[4:5] + tail[5:6]
    for member in range(helpers):
        tail = src_pay[member, block:, :].astype(f32)
        src_value[member : member + 1, :] = tail[0:1] + tail[1:2] + tail[2:3]
        for spot in range(SPOTS):
            own = jnp.where(lane == spot * helpers + here[0], tail[3:4], 0.0)
            bias = jnp.where(jnp.max(own, axis=1, keepdims=True) > 0.5, 0.0, NEGATIVE)
            bias = jnp.broadcast_to(bias, (1, block))
            row_bias[member : member + 1, spot * block : (spot + 1) * block] = bias
            col_bias[spot : spot + 1, member * block : (member + 1) * block] = bias

    def emit(at, row):
        out[pl.ds(at, 1), :] = row

    sweep(src_pay, dst_pay, lambda k: value[k : k + 1, :], row_bias, dots, tops, sums, line, emit)


def later_rows(gathered, dst_value, row_bias, src_pay, dst_pay, out, dots, tops, sums, line, value):
    summed = merged([gathered[k] for k in range(gathered.shape[0])])
    value[...] = jnp.where(summed > 0.5 * NEGATIVE, dst_value[...] - summed, 0.0)

    def emit(at, row):
        out[pl.ds(at, 1), :] = row

    sweep(src_pay, dst_pay, lambda k: value[k : k + 1, :], row_bias, dots, tops, sums, line, emit)


def columns(last, here, gathered, src_value, col_bias, src_pay, dst_pay, *rest):
    if last:
        halves, out, own_f, padded, dots, tops, sums, line, value = rest
    else:
        out, padded, dots, tops, sums, line, value = rest
    rows = merged([gathered[k] for k in range(gathered.shape[0])])
    value[...] = src_value[...] - rows
    if last:
        mine = lax.broadcasted_iota(jnp.int32, rows.shape, 0) == here[1]
        own = jnp.sum(jnp.where(mine, rows, 0.0), axis=0, keepdims=True)
        own_f[...] = halves[0:1, :] - BACK * own
    total = out.shape[0]
    padded[...] = jnp.full(padded.shape, NEGATIVE, f32)

    def emit(at, row):
        padded[pl.ds(at + total + REACH, 1), :] = row

    sweep(dst_pay, src_pay, lambda k: value[k : k + 1, :], col_bias, dots, tops, sums, line, emit)

    def lay(member, carry):
        if last:
            out[pl.ds(member, 1), :] = padded[pl.ds(member - here[0] + total + SPOTS - 1, 1), :]
        else:
            for spot in range(SPOTS):
                out[member, spot : spot + 1, :] = padded[
                    pl.ds(member - here[0] + spot + total + REACH, 1), :
                ]
        return carry

    lax.fori_loop(0, total, lay, 0)


def finish(gathered, halves, own_g):
    total = gathered.shape[0]
    whole = gathered[...]
    top = jnp.max(whole, axis=0, keepdims=True)
    summed = jnp.sum(jnp.exp2(whole - top), axis=0, keepdims=True)
    own_g[...] = halves[1:2, :] - BACK * log_sum(top, summed)


SMEM = pl.BlockSpec(memory_space=pltpu.SMEM)
VMEM = pl.BlockSpec(memory_space=pltpu.VMEM)


def shifted(block, distance):
    devices = range(lax.axis_size("pts"))
    route = [(i - distance, i) for i in devices if i - distance in devices]
    return lax.ppermute(block, "pts", route)


def spread(block):
    nearby = {0: block}
    for heading in (1, -1):
        filled = 1
        while filled < REACH + 1:
            amount = min(filled, REACH + 1 - filled)
            sent = jnp.stack([nearby[-heading * member] for member in range(amount)])
            arrived = shifted(sent, heading * filled)
            for member in range(amount):
                nearby[-heading * (member + filled)] = arrived[member]
            filled += amount
    return jnp.stack([nearby[offset] for offset in range(-REACH, REACH + 1)])


def on_device(src_points, dst_points, src_logw, dst_logw, init_g, pair_lists, pair_counts):
    helpers = lax.axis_size("help")
    total = lax.axis_size("pts")
    pts_here = lax.axis_index("pts").astype(jnp.int32)
    helper_here = lax.axis_index("help").astype(jnp.int32)
    block, width = src_points.shape
    shape = jax.ShapeDtypeStruct
    pay = shape((block + TAIL, width), bf16)
    src_pay, dst_pay, halves = pl.pallas_call(
        prepare,
        out_shape=(pay, pay, shape((2, block), f32)),
        in_specs=[SMEM, SMEM, SMEM] + [VMEM] * 5,
        out_specs=(VMEM,) * 3,
    )(
        ((pts_here - REACH) * helpers)[None],
        pair_lists,
        pair_counts,
        src_points,
        dst_points,
        src_logw[None],
        dst_logw[None],
        init_g[None],
    )
    dst_near = spread(dst_pay)
    src_near = lax.all_gather(src_pay, "help")

    def scratch(row_blocks, col_blocks):
        return [
            pltpu.VMEM((block, col_blocks * block), f32),
            pltpu.VMEM((block, LANES), f32),
            pltpu.VMEM((block, LANES), f32),
            pltpu.VMEM((1, col_blocks * block), f32),
            pltpu.VMEM((col_blocks, block), f32),
        ]

    where_here = jnp.stack([pts_here, helper_here])
    rows_shape = shape((helpers, block), f32)
    row_part, row_bias, col_bias, src_value, dst_value = pl.pallas_call(
        first_rows,
        out_shape=(
            rows_shape,
            shape((helpers, SPOTS * block), f32),
            shape((SPOTS, helpers * block), f32),
            rows_shape,
            shape((SPOTS, block), f32),
        ),
        in_specs=[SMEM, VMEM, VMEM],
        out_specs=(VMEM,) * 5,
        scratch_shapes=scratch(helpers, SPOTS),
    )(helper_here[None], src_near, dst_near)
    padded = pltpu.VMEM((2 * total + 2 * SPOTS, block), f32)
    gathered = lax.all_gather(row_part, "help")
    col_part = pl.pallas_call(
        functools.partial(columns, False),
        out_shape=shape((total, SPOTS, block), f32),
        in_specs=[SMEM] + [VMEM] * 5,
        out_specs=VMEM,
        scratch_shapes=[padded] + scratch(SPOTS, helpers),
    )(where_here, gathered, src_value, col_bias, src_near, dst_near)
    col_all = lax.all_to_all(col_part, "pts", 0, 0)
    row_part = pl.pallas_call(
        later_rows,
        out_shape=rows_shape,
        in_specs=[VMEM] * 5,
        out_specs=VMEM,
        scratch_shapes=scratch(helpers, SPOTS),
    )(col_all, dst_value, row_bias, src_near, dst_near)
    gathered = lax.all_gather(row_part, "help")
    col_part, own_f = pl.pallas_call(
        functools.partial(columns, True),
        out_shape=(shape((total, block), f32), shape((1, block), f32)),
        in_specs=[SMEM] + [VMEM] * 6,
        out_specs=(VMEM, VMEM),
        scratch_shapes=[padded] + scratch(SPOTS, helpers),
    )(where_here, gathered, src_value, col_bias, src_near, dst_near, halves)
    col_all = lax.all_to_all(col_part, "pts", 0, 0)
    own_g = pl.pallas_call(
        finish,
        out_shape=shape((1, block), f32),
        in_specs=[VMEM, VMEM],
        out_specs=VMEM,
    )(col_all, halves)
    return (own_f[0], own_g[0])


def solution(mesh):
    both = ("pts", "help")
    placed = (P(both, None), P(both, None), P(both), P(both), P(both), P(both, None), P(both))
    return jax.shard_map(
        on_device,
        mesh=mesh,
        in_specs=placed,
        out_specs=(P(both), P(both)),
        check_vma=False,
    )
```

time: 591 us -> 109 us (0.18)
  loops' own time: 185 us -> 0 us
  starting transfers between devices: 127 us -> 11.7 us
  matrix products: 108 us -> 0 us
  other arithmetic: 40.9 us -> 1.56 us
  local copies, waits for them, and re-layouts: 42 us -> 3.2 us
  Pallas kernels: 0 us -> 36.2 us
  waiting for transfers between devices: 39.6 us -> 14.4 us
    another operation x6 -> x0, loops' own time: 185 us -> none  [the longest x2 93.4 us: on_device(): lax.scan(column_step, initial, (pair_spots, pair_rows, pair_active, stored))]
    ppermute x42 -> x4, starting transfers between devices: 127 us -> 11.7 us  [shifted(): return lax.ppermute(block, 'pts', route)]
    dot_general x96 -> x0, matrix products: 108 us -> none  [inner_tile(): lax.dot_general(lefts[member], rights[member], (((1,), (1,)), ((), ())),...]
    pallas_call x0 -> x6, Pallas kernels: none -> 36.2 us  [the longest x1 9.22 us: on_device(): pl.pallas_call(functools.partial(columns, False), out_shape=shape((total,...]
    slice x54 -> x0, local copies, waits for them, and re-layouts: 26.5 us -> none  [the longest x48 26.4 us: pick_two(): index_pair[member]]
    ppermute x42 -> x4, waiting for transfers between devices: 39.6 us -> 14.4 us  [shifted(): return lax.ppermute(block, 'pts', route)]
    all_gather x7 -> x3, blocking collectives: 40.3 us -> 19.9 us  [the longest x2 12.1 us: on_device(): gathered = lax.all_gather(row_part, 'help')]
    all_to_all x0 -> x2, blocking collectives: none -> 19.8 us  [on_device(): col_all = lax.all_to_all(col_part, 'pts', 0, 0)]
  transfers between devices with their start and end apart: 42 -> 4, of which waited for: 7 -> 3; matrix products, arithmetic and copies ran while one was open for 2% -> 1% of each run, Pallas kernels for 0% -> 0%
where the time goes in v1:
time: 109 us; the launch traced here: 108 us
  blocking collectives  39.8 us (37%)
  Pallas kernels  36.2 us (33%)
  waiting for transfers between devices  14.4 us (13%)
  starting transfers between devices  11.7 us (11%)
  local copies, waits for them, and re-layouts  3.2 us (3%)
  other arithmetic  1.56 us (1%)
  between operations  1.4 us (1%)
    all_to_all x2, blocking collectives, on_device(): col_all = lax.all_to_all(col_part, 'pts', 0, 0)  19.8 us
    ppermute x4, waiting for transfers between devices, shifted(): return lax.ppermute(block, 'pts', route)  14.4 us
    all_gather x2, blocking collectives, on_device(): gathered = lax.all_gather(row_part, 'help')  12.1 us
    ppermute x4, starting transfers between devices, shifted(): return lax.ppermute(block, 'pts', route)  11.7 us
    pallas_call x1, Pallas kernels, on_device(): pl.pallas_call(functools.partial(columns, False), out_shape=shape((total,...  9.22 us
    pallas_call x1, Pallas kernels, on_device(): pl.pallas_call(functools.partial(columns, True), out_shape=(shape((total,...  9.1 us
    all_gather x1, blocking collectives, on_device(): src_near = lax.all_gather(src_pay, 'help')  7.81 us
    pallas_call x1, Pallas kernels, on_device(): pl.pallas_call(first_rows, out_shape=(rows_shape, shape((helpers, SPOTS *...  7.35 us
  transfers between devices with their start and end apart: 4, of which 3 were waited for; matrix products, arithmetic and copies ran while one was open for 1% of the time, Pallas kernels for 0%

profile of v1, /device:TPU:0, one launch (start us, length us, event | category | flops | bytes accessed | tf_op | source)
XLA Modules:
  0.0 108.3 jit_solution(1744382709589641641)
XLA Ops:
  1.3 1.9 %shard_map.86 = (bf16[272,256]{1,0:T(8,128)(2,1)}, bf16[272,256]{1,0:T(8,128)(2,1)}, f32[2,256]{1,0:T(2,128)}) custom-call(s32[1]{0:T(128)} %bitcast.2.base, s32[1,24]{1,0:T(1,128)} %lists.1, s32[1]{0:T(128)S(6)} %copy.18.counts, bf16[256,256]{1,0:T(8,128)(2,1)} %src.1, bf16[256,256]{1,0:T(8,128)(2,1)} %dst.1, f32[1,256]{1,0:T(1,128)} %bitcast.28, ...), custom_call_target="tpu_custom_call" | custom-call | tf_op jit(solution)/shard_map/pallas_call | solution.py:230
  3.2 4.9 %collective-permute-start = (bf16[1,272,256]{2,1,0:T(8,128)(2,1)}, bf16[1,272,256]{2,1,0:T(8,128)(2,1)S(1)}, u32[]{:S(2)}, u32[]{:S(2)}) collective-permute-start(bf16[1,272,256]{2,1,0:T(8,128)(2,1)} %bitcast.21), channel_id=1, source_target_pairs={{0,4},{4,8},{8,12},{12,16},{16,20},{20,24},{24,28},{1,5},{5,9},{9,... | collective-permute-start | bytes 417800 | tf_op jit(solution)/shard_map/ppermute | solution.py:205
  8.1 1.3 %collective-permute-start.2 = (bf16[1,272,256]{2,1,0:T(8,128)(2,1)}, bf16[1,272,256]{2,1,0:T(8,128)(2,1)S(1)}, u32[]{:S(2)}, u32[]{:S(2)}) collective-permute-start(bf16[1,272,256]{2,1,0:T(8,128)(2,1)} %bitcast.22), channel_id=1, source_target_pairs={{4,0},{8,4},{12,8},{16,12},{20,16},{24,20},{28,24},{5,1},{9,5},{13... | collective-permute-start | bytes 417800 | tf_op jit(solution)/shard_map/ppermute | solution.py:205
  9.4 0.0 copy-start.2
  9.4 1.9 %collective-permute-done = bf16[1,272,256]{2,1,0:T(8,128)(2,1)S(1)} collective-permute-done((bf16[1,272,256]{2,1,0:T(8,128)(2,1)}, bf16[1,272,256]{2,1,0:T(8,128)(2,1)S(1)}, u32[]{:S(2)}, u32[]{:S(2)}) %collective-permute-start) | collective-permute-done | bytes 139296 | tf_op jit(solution)/shard_map/ppermute | solution.py:205
  11.3 4.0 %collective-permute-done.2 = bf16[1,272,256]{2,1,0:T(8,128)(2,1)S(1)} collective-permute-done((bf16[1,272,256]{2,1,0:T(8,128)(2,1)}, bf16[1,272,256]{2,1,0:T(8,128)(2,1)S(1)}, u32[]{:S(2)}, u32[]{:S(2)}) %collective-permute-start.2) | collective-permute-done | bytes 139296 | tf_op jit(solution)/shard_map/ppermute | solution.py:205
  15.3 0.9 pad_maximum_fusion
  16.3 4.3 %collective-permute-start.1 = (bf16[2,272,256]{2,1,0:T(8,128)(2,1)S(1)}, bf16[2,272,256]{2,1,0:T(8,128)(2,1)S(1)}, u32[]{:S(2)}, u32[]{:S(2)}) collective-permute-start(bf16[2,272,256]{2,1,0:T(8,128)(2,1)S(1)} %get-tuple-element.23), channel_id=1, source_target_pairs={{0,8},{4,12},{8,16},{12,20},{16,24},{20,28},{1,9},{5,13},{9,17},{1... | collective-permute-start | bytes 835592 | tf_op jit(solution)/shard_map/ppermute | solution.py:205
  20.6 0.6 pad_add_fusion.here
  21.2 0.0 copy-done.2
  21.2 7.8 %all-gather = bf16[1088,256]{1,0:T(8,128)(2,1)} all-gather(bf16[272,256]{1,0:T(8,128)(2,1)S(1)} %copy-done.2), channel_id=2, replica_groups=mesh['pts'=8,'help'=4] {'help'}, dimensions={0}, use_global_device_ids=true | all-gather | bytes 696320 | tf_op jit(solution)/shard_map/all_gather | solution.py:246
  29.0 1.3 %collective-permute-start.3 = (bf16[2,272,256]{2,1,0:T(8,128)(2,1)S(1)}, bf16[2,272,256]{2,1,0:T(8,128)(2,1)S(1)}, u32[]{:S(2)}, u32[]{:S(2)}) collective-permute-start(bf16[2,272,256]{2,1,0:T(8,128)(2,1)S(1)} %get-tuple-element.22), channel_id=1, source_target_pairs={{8,0},{12,4},{16,8},{20,12},{24,16},{28,20},{9,1},{13,5},{17,9},{2... | collective-permute-start | bytes 835592 | tf_op jit(solution)/shard_map/ppermute | solution.py:205
  30.3 0.0 collective-permute-done.1
  30.3 0.0 copy-start.1
  30.3 0.9 copy-done.1
  31.3 8.5 %collective-permute-done.3 = bf16[2,272,256]{2,1,0:T(8,128)(2,1)S(1)} collective-permute-done((bf16[2,272,256]{2,1,0:T(8,128)(2,1)S(1)}, bf16[2,272,256]{2,1,0:T(8,128)(2,1)S(1)}, u32[]{:S(2)}, u32[]{:S(2)}) %collective-permute-start.3) | collective-permute-done | bytes 278560 | tf_op jit(solution)/shard_map/ppermute | solution.py:205
  39.8 0.0 copy-start
  39.8 0.9 copy-done
  40.7 7.4 %shard_map.87 = (f32[4,256]{1,0:T(4,128)}, f32[4,1792]{1,0:T(4,128)}, f32[7,1024]{1,0:T(8,128)}, f32[4,256]{1,0:T(4,128)}, f32[7,256]{1,0:T(8,128)}) custom-call(s32[1]{0:T(128)} %bitcast.1.here, bf16[4,272,256]{2,1,0:T(8,128)(2,1)} %bitcast.17, bf16[7,272,256]{2,1,0:T(8,128)(2,1)} %copy-done), custom_call_target="tpu_custom_call" | custom-call | tf_op jit(solution)/shard_map/pallas_call | solution.py:259
  48.1 5.8 %all-gather.3.gathered = f32[4,4,256]{2,1,0:T(4,128)} all-gather(f32[1,4,256]{2,1,0:T(4,128)} %bitcast.27), channel_id=3, replica_groups=mesh['pts'=8,'help'=4] {'help'}, dimensions={0}, use_global_device_ids=true | all-gather | bytes 20480 | tf_op jit(solution)/shard_map/all_gather | solution.py:273
  53.9 9.2 %shard_map.88 = f32[8,7,256]{2,1,0:T(8,128)} custom-call(s32[2]{0:T(128)} %pad_add_fusion.here, f32[4,4,256]{2,1,0:T(4,128)} %all-gather.3.gathered, f32[4,256]{1,0:T(4,128)} %get-tuple-element.15.src_value, f32[7,1024]{1,0:T(8,128)} %get-tuple-element.16.col_bias, bf16[4,272,256]{2,1,0:T(8,128)(2,1)} %bitcast.18, bf16[7,272,256]{2,1,0:T(8,128)(2,1)} %copy-done), custom_call_target="tpu_custom_call" | custom-call | tf_op jit(solution)/shard_map/pallas_call | solution.py:274
  63.1 11.0 %all_to_all.16.gathered = f32[8,7,256]{2,1,0:T(8,128)} all-to-all(f32[8,7,256]{2,1,0:T(8,128)} %shard_map.88), channel_id=1, replica_groups=mesh['pts'=8,'help'=4] {'pts'}, dimensions={0} | all-to-all | bytes 114688 | tf_op jit(solution)/shard_map/all_to_all | solution.py:281
  74.1 7.3 %shard_map.89 = f32[4,256]{1,0:T(4,128)} custom-call(f32[8,7,256]{2,1,0:T(8,128)} %all_to_all.16.gathered, f32[7,256]{1,0:T(8,128)} %get-tuple-element.17.dst_value, f32[4,1792]{1,0:T(4,128)} %get-tuple-element.18.row_bias, bf16[4,272,256]{2,1,0:T(8,128)(2,1)} %bitcast.19, bf16[7,272,256]{2,1,0:T(8,128)(2,1)} %copy-done), custom_call_target="tpu_custom_call" | custom-call | tf_op jit(solution)/shard_map/pallas_call | solution.py:282
  81.4 6.3 %all-gather.4.gathered = f32[4,4,256]{2,1,0:T(4,128)} all-gather(f32[1,4,256]{2,1,0:T(4,128)} %bitcast.25), channel_id=4, replica_groups=mesh['pts'=8,'help'=4] {'help'}, dimensions={0}, use_global_device_ids=true | all-gather | bytes 20480 | tf_op jit(solution)/shard_map/all_gather | solution.py:289
  87.7 9.1 %shard_map.90 = (f32[8,256]{1,0:T(8,128)}, f32[1,256]{1,0:T(1,128)}) custom-call(s32[2]{0:T(128)} %pad_add_fusion.here, f32[4,4,256]{2,1,0:T(4,128)} %all-gather.4.gathered, f32[4,256]{1,0:T(4,128)} %get-tuple-element.15.src_value, f32[7,1024]{1,0:T(8,128)} %get-tuple-element.16.col_bias, bf16[4,272,256]{2,1,0:T(8,128)(2,1)} %bitcast.20, ...), custom_call_target="tpu_custom_call" | custom-call | tf_op jit(solution)/shard_map/pallas_call | solution.py:290
  96.8 0.7 copy.9
  97.5 8.9 %all_to_all.17 = f32[8,1,256]{2,1,0:T(1,128)S(1)} all-to-all(f32[8,1,256]{2,1,0:T(1,128)S(1)} %copy.9), channel_id=1, replica_groups=mesh['pts'=8,'help'=4] {'pts'}, dimensions={0} | all-to-all | bytes 16384 | tf_op jit(solution)/shard_map/all_to_all | solution.py:297
  106.4 0.6 copy.12
  107.0 1.3 %shard_map.91 = f32[1,256]{1,0:T(1,128)} custom-call(f32[8,256]{1,0:T(8,128)} %bitcast.24, f32[2,256]{1,0:T(2,128)} %get-tuple-element.19.rest_0_.halves), custom_call_target="tpu_custom_call" | custom-call | tf_op jit(solution)/shard_map/pallas_call | solution.py:298
  (6 shorter events, 0.1 us)
Async XLA Ops:
  3.2 8.1 %collective-permute-start = (bf16[1,272,256]{2,1,0:T(8,128)(2,1)}, bf16[1,272,256]{2,1,0:T(8,128)(2,1)S(1)}, u32[]{:S(2)}, u32[]{:S(2)}) collective-permute-start(bf16[1,272,256]{2,1,0:T(8,128)(2,1)} %bitcast.21), channel_id=1, source_target_pairs={{0,4},{4,8},{8,12},{12,16},{16,20},{20,24},{24,28},{1,5},{5,9},{9,... | collective-permute-start | bytes 417800 | tf_op jit(solution)/shard_map/ppermute | solution.py:205
  8.1 7.2 %collective-permute-start.2 = (bf16[1,272,256]{2,1,0:T(8,128)(2,1)}, bf16[1,272,256]{2,1,0:T(8,128)(2,1)S(1)}, u32[]{:S(2)}, u32[]{:S(2)}) collective-permute-start(bf16[1,272,256]{2,1,0:T(8,128)(2,1)} %bitcast.22), channel_id=1, source_target_pairs={{4,0},{8,4},{12,8},{16,12},{20,16},{24,20},{28,24},{5,1},{9,5},{13... | collective-permute-start | bytes 417800 | tf_op jit(solution)/shard_map/ppermute | solution.py:205
  9.4 11.8 %copy-start.2 = (bf16[272,256]{1,0:T(8,128)(2,1)S(1)}, bf16[272,256]{1,0:T(8,128)(2,1)}, u32[]{:S(2)}) copy-start(bf16[272,256]{1,0:T(8,128)(2,1)} %get-tuple-element.12) | copy-start | bytes 417796
  16.3 14.0 %collective-permute-start.1 = (bf16[2,272,256]{2,1,0:T(8,128)(2,1)S(1)}, bf16[2,272,256]{2,1,0:T(8,128)(2,1)S(1)}, u32[]{:S(2)}, u32[]{:S(2)}) collective-permute-start(bf16[2,272,256]{2,1,0:T(8,128)(2,1)S(1)} %get-tuple-element.23), channel_id=1, source_target_pairs={{0,8},{4,12},{8,16},{12,20},{16,24},{20,28},{1,9},{5,13},{9,17},{1... | collective-permute-start | bytes 835592 | tf_op jit(solution)/shard_map/ppermute | solution.py:205
  29.0 10.8 %collective-permute-start.3 = (bf16[2,272,256]{2,1,0:T(8,128)(2,1)S(1)}, bf16[2,272,256]{2,1,0:T(8,128)(2,1)S(1)}, u32[]{:S(2)}, u32[]{:S(2)}) collective-permute-start(bf16[2,272,256]{2,1,0:T(8,128)(2,1)S(1)} %get-tuple-element.22), channel_id=1, source_target_pairs={{8,0},{12,4},{16,8},{20,12},{24,16},{28,20},{9,1},{13,5},{17,9},{2... | collective-permute-start | bytes 835592 | tf_op jit(solution)/shard_map/ppermute | solution.py:205
  30.3 0.9 copy-start.1
  39.8 1.0 copy-start

commit v2 on v1

v2 whole, which is shorter than its diff:
```python
import functools
import math

import jax
import jax.numpy as jnp
from jax import lax
from jax.experimental import pallas as pl
from jax.experimental.pallas import tpu as pltpu
from jax.sharding import PartitionSpec as P

REACH = 3
SPOTS = 2 * REACH + 1
EPS = 0.25
NEGATIVE = -1e30
LOG2E = math.log2(math.e)
SCALE = LOG2E / EPS
BACK = EPS / LOG2E
TAIL = 16
LANES = 128
SUBLANES = 8
CHUNK = 64

f32 = jnp.float32
bf16 = jnp.bfloat16


def pieces(value):
    high = value.astype(bf16).astype(f32)
    rest = value - high
    middle = rest.astype(bf16).astype(f32)
    low = (rest - middle).astype(bf16).astype(f32)
    return [high, middle, low]


def stacked(rows, width):
    index = lax.broadcasted_iota(jnp.int32, (TAIL, width), 0)
    out = jnp.zeros((TAIL, width), f32)
    for at, row in enumerate(rows):
        out = jnp.where(index == at, row, out)
    return out.astype(bf16)


def half_norms(points):
    wide = points.astype(f32)
    square = wide * wide
    high = square.astype(bf16)
    low = (square - high.astype(f32)).astype(bf16)
    ones = jnp.ones((8, points.shape[1]), bf16)
    dims = (((1,), (1,)), ((), ()))
    total = lax.dot_general(ones, high, dims, preferred_element_type=f32) + lax.dot_general(
        ones, low, dims, preferred_element_type=f32
    )
    return 0.5 * total[0:1]


def log_sum(top, values):
    return top + jnp.log(values) * LOG2E


def merged(parts):
    top = functools.reduce(jnp.maximum, parts)
    return log_sum(top, sum(jnp.exp2(part - top) for part in parts))


def swap_route(size, step):
    if size & (size - 1) == 0:
        return [(i, i ^ step) for i in range(size)]
    return [((i + step) % size, i) for i in range(size)]


def swap_slot(size, slot, step):
    return slot ^ step if size & (size - 1) == 0 else (slot - step) % size


def exchanges(total):
    if total & (total - 1) == 0:
        steps = [k for k in range(1, total) if any(abs(i - (i ^ k)) <= REACH for i in range(total))]
        if len(steps) <= 2 * REACH:
            return [("xor", step, 0) for step in steps]
    return [("pair", far, turn) for far in range(1, REACH + 1) for turn in range(2)]


def partner(exchange, index):
    kind, step, turn = exchange
    if kind == "xor":
        return index ^ step
    ahead = (index // step) % 2 == turn
    if isinstance(index, int):
        return index + step if ahead else index - step
    return jnp.where(ahead, index + step, index - step)


def prepare(here, lists, counts, src, dst, src_lw, dst_lw, start, src_pay, dst_pay, halves):
    block, width = src.shape
    dst_half = half_norms(dst[...])
    weight = dst_lw[...] * LOG2E
    first = weight + (start[...] - dst_half) * SCALE
    dst_pay[0:block, :] = dst[...]
    dst_pay[block:, :] = stacked(pieces(first) + pieces(weight), width)
    lane = lax.broadcasted_iota(jnp.int32, (1, width), 1) + (here[0] - REACH) * here[2]
    count = counts[0]
    paired = jnp.zeros((1, width), f32)
    for entry in range(lists.shape[1]):
        column = jnp.where(entry < count, lists[0, entry], lists[0, 0])
        paired = jnp.where(lane == column, 1.0, paired)
    src_pay[0:block, :] = src[...]
    src_pay[block:, :] = stacked(pieces(src_lw[...] * LOG2E) + [paired], width)
    halves[0:1, :] = half_norms(src[...])
    halves[1:2, :] = dst_half


def product(left, right, block):
    return lax.dot_general(
        left[0:block, :], right[0:block, :], (((1,), (1,)), ((), ())), preferred_element_type=f32
    )


def row_sums(src, dst, values, bias, out, dots, tops, sums):
    block = tops.shape[1]

    def multiply(at):
        for k, cols in enumerate(dst):
            dots[at % 2, :, k * block : (k + 1) * block] = product(src[at], cols, block)

    multiply(0)
    for at in range(len(src)):
        if at + 1 < len(src):
            multiply(at + 1)
        slot = at % 2
        lines = []
        for k, value in enumerate(values):
            line = value + bias[at : at + 1, k * block : (k + 1) * block]
            lines += [
                jnp.broadcast_to(line[:, lane : lane + LANES], (SUBLANES, LANES))
                for lane in range(0, block, LANES)
            ]
        for row in range(0, block, SUBLANES):
            parts = [
                dots[slot, row : row + SUBLANES, k * LANES : (k + 1) * LANES] * SCALE + line
                for k, line in enumerate(lines)
            ]
            top = functools.reduce(jnp.maximum, parts)
            tops[slot, row : row + SUBLANES, :] = top
            sums[slot, row : row + SUBLANES, :] = sum(jnp.exp2(part - top) for part in parts)
        turned = tops[slot].T
        peak = jnp.max(turned, axis=0, keepdims=True)
        total = jnp.sum(sums[slot].T * jnp.exp2(turned - peak), axis=0, keepdims=True)
        out[at : at + 1, :] = log_sum(peak, total)


def column_sums(src, dst, values, bias, dots, spread, emit):
    block = values[0].shape[1]
    for k, value in enumerate(values):
        spread[k * block : (k + 1) * block, :] = jnp.broadcast_to(value, (LANES, block)).T

    def multiply(at):
        for k, rows in enumerate(src):
            dots[at % 2, k * block : (k + 1) * block, :] = product(rows, dst[at], block)

    multiply(0)
    for at in range(len(dst)):
        if at + 1 < len(dst):
            multiply(at + 1)
        slot = at % 2
        halves = []
        for lane in range(0, block, LANES):
            found = []
            for k in range(len(src)):
                top = summed = None
                for first in range(k * block, (k + 1) * block, CHUNK):
                    parts = [
                        dots[slot, row : row + SUBLANES, lane : lane + LANES] * SCALE
                        + spread[row : row + SUBLANES, :]
                        for row in range(first, first + CHUNK, SUBLANES)
                    ]
                    peak = functools.reduce(jnp.maximum, parts)
                    if top is None:
                        top = peak
                        summed = sum(jnp.exp2(part - top) for part in parts)
                    else:
                        higher = jnp.maximum(top, peak)
                        summed = summed * jnp.exp2(top - higher) + sum(
                            jnp.exp2(part - higher) for part in parts
                        )
                        top = higher
                at_lane = k * block + lane
                found.append((top + bias[at : at + 1, at_lane : at_lane + LANES], summed))
            peak = functools.reduce(jnp.maximum, [top for top, _ in found])
            summed = sum(part * jnp.exp2(top - peak) for top, part in found)
            highest = jnp.max(peak, axis=0, keepdims=True)
            total = jnp.sum(summed * jnp.exp2(peak - highest), axis=0, keepdims=True)
            halves.append(log_sum(highest, total))
        emit(at, jnp.concatenate(halves, axis=1))


def first_rows(routes, here, *refs):
    helpers = here_helpers(refs, routes)
    spots = len(routes) + 1
    src, refs = refs[:helpers], refs[helpers:]
    dst, refs = refs[:spots], refs[spots:]
    out, row_bias, col_bias, src_value, dst_value, dots, tops, sums = refs
    block = tops.shape[1]
    lane = lax.broadcasted_iota(jnp.int32, (1, src[0].shape[1]), 1)
    values = []
    for spot in range(spots):
        tail = dst[spot][block:, :].astype(f32)
        values.append(tail[0:1] + tail[1:2] + tail[2:3])
        dst_value[spot : spot + 1, :] = tail[3:4] + tail[4:5] + tail[5:6]
    groups = [here[0]] + [partner(route, here[0]) for route in routes]
    for member in range(helpers):
        tail = src[member][block:, :].astype(f32)
        src_value[member : member + 1, :] = tail[0:1] + tail[1:2] + tail[2:3]
        for spot, group in enumerate(groups):
            wanted = (group - here[0] + REACH) * here[2] + here[1]
            own = jnp.where(lane == wanted, tail[3:4], 0.0)
            own = jnp.where(jnp.max(own, axis=1, keepdims=True) > 0.5, 0.0, NEGATIVE)
            own = jnp.broadcast_to(own, (1, block))
            row_bias[member : member + 1, spot * block : (spot + 1) * block] = own
            col_bias[spot : spot + 1, member * block : (member + 1) * block] = own
    row_sums(src, dst, values, row_bias, out, dots, tops, sums)


def here_helpers(refs, routes):
    return len(refs) - (len(routes) + 1) - 8


def later_rows(helpers, gathered, dst_value, row_bias, *refs):
    src, refs = refs[:helpers], refs[helpers:]
    dst, (out, dots, tops, sums) = refs[:-4], refs[-4:]
    summed = merged([gathered[k] for k in range(gathered.shape[0])])
    value = jnp.where(summed > 0.5 * NEGATIVE, dst_value[...] - summed, 0.0)
    values = [value[k : k + 1, :] for k in range(len(dst))]
    row_sums(src, dst, values, row_bias, out, dots, tops, sums)


def columns(last, routes, helpers, here, src_value, col_bias, *refs):
    spots = len(routes) + 1
    given, refs = refs[:helpers], refs[helpers:]
    src, refs = refs[:helpers], refs[helpers:]
    dst, refs = refs[:spots], refs[spots:]
    if last:
        halves, out, own_f, padded, dots, spread = refs
    else:
        out, padded, dots, spread = refs
    values = []
    for member in range(helpers):
        summed = merged(
            [
                given[step][(place := swap_slot(helpers, member, step)) : place + 1, :]
                for step in range(helpers)
            ]
        )
        values.append(src_value[member : member + 1, :] - summed)
        if last and member == 0:
            own_f[...] = halves[0:1, :] - BACK * summed
    total = out.shape[0]
    middle = total + SPOTS
    padded[...] = jnp.full(padded.shape, NEGATIVE, f32)
    groups = [here[0]] + [partner(route, here[0]) for route in routes]

    def emit(at, row):
        padded[pl.ds(groups[at] - here[0] + middle, 1), :] = row

    column_sums(src, dst, values, col_bias, dots, spread, emit)

    def lay(member, carry):
        if last:
            out[member] = padded[pl.ds(member - here[0] + middle, 1), :]
        else:
            wanted = [member] + [partner(route, member) for route in routes]
            for spot, group in enumerate(wanted):
                out[member, spot : spot + 1, :] = padded[pl.ds(group - here[0] + middle, 1), :]
        return carry

    lax.fori_loop(0, total, lay, 0)


def finish(gathered, halves, own_g):
    summed = merged([gathered[k] for k in range(gathered.shape[0])])
    own_g[...] = halves[1:2, :] - BACK * summed


SMEM = pl.BlockSpec(memory_space=pltpu.SMEM)
VMEM = pl.BlockSpec(memory_space=pltpu.VMEM)
PARAMS = pltpu.CompilerParams(vmem_limit_bytes=20 * 1024 * 1024)


def kernel(body, out_shape, ins, scratch=()):
    several = isinstance(out_shape, tuple)
    return pl.pallas_call(
        body,
        out_shape=out_shape,
        in_specs=ins,
        out_specs=(VMEM,) * len(out_shape) if several else VMEM,
        scratch_shapes=list(scratch),
        compiler_params=PARAMS,
    )


def on_device(src_points, dst_points, src_logw, dst_logw, init_g, pair_lists, pair_counts):
    helpers = lax.axis_size("help")
    total = lax.axis_size("pts")
    here = jnp.stack(
        [
            lax.axis_index("pts").astype(jnp.int32),
            lax.axis_index("help").astype(jnp.int32),
            jnp.int32(helpers),
        ]
    )
    block, width = src_points.shape
    routes = exchanges(total)
    spots = len(routes) + 1
    shape = jax.ShapeDtypeStruct
    pay = shape((block + TAIL, width), bf16)
    src_pay, dst_pay, halves = kernel(
        prepare, (pay, pay, shape((2, block), f32)), [SMEM] * 3 + [VMEM] * 5
    )(
        here,
        pair_lists,
        pair_counts,
        src_points,
        dst_points,
        src_logw[None],
        dst_logw[None],
        init_g[None],
    )
    dst = [dst_pay]
    for route in routes:
        ends = [(i, partner(route, i)) for i in range(total)]
        ends = [(i, j) for i, j in ends if 0 <= j < total]
        dst.append(lax.ppermute(dst_pay, "pts", ends))

    def traded(value):
        return [value] + [
            lax.ppermute(value, "help", swap_route(helpers, step)) for step in range(1, helpers)
        ]

    src = traded(src_pay)
    row_scratch = [
        pltpu.VMEM((2, block, spots * block), f32),
        pltpu.VMEM((2, block, LANES), f32),
        pltpu.VMEM((2, block, LANES), f32),
    ]
    col_scratch = [
        pltpu.VMEM((2 * total + 2 * SPOTS, block), f32),
        pltpu.VMEM((2, helpers * block, block), f32),
        pltpu.VMEM((helpers * block, LANES), f32),
    ]
    rows_shape = shape((helpers, block), f32)
    row_part, row_bias, col_bias, src_value, dst_value = kernel(
        functools.partial(first_rows, routes),
        (
            rows_shape,
            shape((helpers, spots * block), f32),
            shape((spots, helpers * block), f32),
            rows_shape,
            shape((spots, block), f32),
        ),
        [SMEM] + [VMEM] * (helpers + spots),
        row_scratch,
    )(here, *src, *dst)
    col_part = kernel(
        functools.partial(columns, False, routes, helpers),
        shape((total, spots, block), f32),
        [SMEM] + [VMEM] * (2 + 2 * helpers + spots),
        col_scratch,
    )(here, src_value, col_bias, *traded(row_part), *src, *dst)
    col_all = lax.all_to_all(col_part, "pts", 0, 0)
    row_part = kernel(
        functools.partial(later_rows, helpers),
        rows_shape,
        [VMEM] * (3 + helpers + spots),
        row_scratch,
    )(col_all, dst_value, row_bias, *src, *dst)
    col_part, own_f = kernel(
        functools.partial(columns, True, routes, helpers),
        (shape((total, 1, block), f32), shape((1, block), f32)),
        [SMEM] + [VMEM] * (3 + 2 * helpers + spots),
        col_scratch,
    )(here, src_value, col_bias, *traded(row_part), *src, *dst, halves)
    col_all = lax.all_to_all(col_part, "pts", 0, 0)
    own_g = kernel(finish, shape((1, block), f32), [VMEM, VMEM])(col_all, halves)
    return (own_f[0], own_g[0])


def solution(mesh):
    both = ("pts", "help")
    placed = (P(both, None), P(both, None), P(both), P(both), P(both), P(both, None), P(both))
    return jax.shard_map(
        on_device,
        mesh=mesh,
        in_specs=placed,
        out_specs=(P(both), P(both)),
        check_vma=False,
    )
```

time: 109 us -> 72.1 us (0.66)
  Pallas kernels: 36.2 us -> 13 us
  blocking collectives: 39.8 us -> 21.2 us
  starting transfers between devices: 11.7 us -> 18.3 us
  other arithmetic: 1.56 us -> 0.08 us
  waiting for transfers between devices: 14.4 us -> 15.5 us
    pallas_call x6, Pallas kernels: 36.2 us -> 13 us  [the longest x1 3.44 us: on_device(): kernel(functools.partial(columns, True, routes, helpers), (shape((total,...]
    all_gather x3 -> x0, blocking collectives: 19.9 us -> none  [the longest x2 12.1 us: on_device(): gathered = lax.all_gather(row_part, 'help')]
    ppermute x4 -> x15, starting transfers between devices: 11.7 us -> 18.3 us  [the longest x6 11.3 us: on_device(): dst.append(lax.ppermute(dst_pay, 'pts', ends))]
    another operation x2 -> x1, other arithmetic: 1.56 us -> 0.08 us  [on_device(): jnp.stack([lax.axis_index('pts').astype(jnp.int32), lax.axis_index('help'...]
    all_to_all x2, blocking collectives: 19.8 us -> 21.2 us  [on_device(): col_all = lax.all_to_all(col_part, 'pts', 0, 0)]
    ppermute x4 -> x15, waiting for transfers between devices: 14.4 us -> 15.5 us  [the longest x6 11.6 us: on_device(): dst.append(lax.ppermute(dst_pay, 'pts', ends))]
  transfers between devices with their start and end apart: 4 -> 15, of which waited for: 3 -> 6; matrix products, arithmetic and copies ran while one was open for 1% -> 0% of each run, Pallas kernels for 0% -> 0%
where the time goes in v2:
time: 72.1 us; the launch traced here: 71.8 us
  blocking collectives  21.2 us (29%)
  starting transfers between devices  18.3 us (25%)
  waiting for transfers between devices  15.5 us (21%)
  Pallas kernels  13 us (18%)
  local copies, waits for them, and re-layouts  2.51 us (3%)
  between operations  1.33 us (2%)
    all_to_all x2, blocking collectives, on_device(): col_all = lax.all_to_all(col_part, 'pts', 0, 0)  21.2 us
    ppermute x6, waiting for transfers between devices, on_device(): dst.append(lax.ppermute(dst_pay, 'pts', ends))  11.6 us
    ppermute x6, starting transfers between devices, on_device(): dst.append(lax.ppermute(dst_pay, 'pts', ends))  11.3 us
    ppermute x9, starting transfers between devices, traded(): lax.ppermute(value, 'help', swap_route(helpers, step))  7.02 us
    ppermute x9, waiting for transfers between devices, traded(): lax.ppermute(value, 'help', swap_route(helpers, step))  3.84 us
    pallas_call x1, Pallas kernels, on_device(): kernel(functools.partial(columns, True, routes, helpers), (shape((total,...  3.44 us
    pallas_call x1, Pallas kernels, on_device(): kernel(functools.partial(columns, False, routes, helpers), shape((total,...  2.95 us
    pallas_call x1, Pallas kernels, on_device(): kernel(functools.partial(first_rows, routes), (rows_shape, shape((helpers...  2.88 us
  transfers between devices with their start and end apart: 15, of which 6 were waited for; matrix products, arithmetic and copies ran while one was open for 0% of the time, Pallas kernels for 0%

profile of v2, /device:TPU:0, one launch (start us, length us, event | category | flops | bytes accessed | tf_op | source)
XLA Modules:
  0.0 71.8 jit_solution(10711497224678501385)
XLA Ops:
  1.3 0.1 pad_add_fusion.here
  1.4 0.7 copy-done.3
  2.1 0.9 %copy-done = bf16[256,256]{1,0:T(8,128)(2,1)S(1)} copy-done((bf16[256,256]{1,0:T(8,128)(2,1)S(1)}, bf16[256,256]{1,0:T(8,128)(2,1)}, u32[]{:S(2)}) %copy-start) | copy-done | bytes 131096
  3.0 0.9 %copy-done.1 = bf16[256,256]{1,0:T(8,128)(2,1)S(1)} copy-done((bf16[256,256]{1,0:T(8,128)(2,1)S(1)}, bf16[256,256]{1,0:T(8,128)(2,1)}, u32[]{:S(2)}) %copy-start.1) | copy-done | bytes 131096
  3.9 0.8 %shard_map.86 = (bf16[272,256]{1,0:T(8,128)(2,1)S(1)}, bf16[272,256]{1,0:T(8,128)(2,1)S(1)}, f32[2,256]{1,0:T(2,128)S(1)}) custom-call(s32[3]{0:T(128)S(1)} %pad_add_fusion.here, s32[1,24]{1,0:T(1,128)S(1)} %copy-done.5, s32[1]{0:T(128)S(6)} %copy.9.counts, bf16[256,256]{1,0:T(8,128)(2,1)S(1)} %copy-done, bf16[256,256]{1,0:T(8,128)(2,1)S(1)} %copy-done.1, ...), custom_call_target="tpu_custom_call" | custom-call | tf_op jit(solution)/shard_map/pallas_call | solution.py:315
  4.7 2.5 %collective-permute-start.2 = (bf16[272,256]{1,0:T(8,128)(2,1)S(1)}, bf16[272,256]{1,0:T(8,128)(2,1)S(1)}, u32[]{:S(2)}, u32[]{:S(2)}) collective-permute-start(bf16[272,256]{1,0:T(8,128)(2,1)S(1)} %get-tuple-element.12.refs_0_.refs_4_), channel_id=1, source_target_pairs={{0,3},{1,2},{2,1},{3,0},{4,7},{5,6},{6,5},{7,4},{8,11},{9,10},{10,... | collective-permute-start | bytes 417800 | tf_op jit(solution)/shard_map/ppermute | solution.py:335
  7.2 0.6 collective-permute-start.1
  7.9 4.8 %collective-permute-start.8 = (bf16[272,256]{1,0:T(8,128)(2,1)S(1)}, bf16[272,256]{1,0:T(8,128)(2,1)S(1)}, u32[]{:S(2)}, u32[]{:S(2)}) collective-permute-start(bf16[272,256]{1,0:T(8,128)(2,1)S(1)} %get-tuple-element.13.refs_4_.refs_8_), channel_id=1, source_target_pairs={{0,28},{4,24},{8,20},{12,16},{16,12},{20,8},{24,4},{28,0},{1,29},{... | collective-permute-start | bytes 417800 | tf_op jit(solution)/shard_map/ppermute | solution.py:331
  12.7 0.2 collective-permute-start.7
  12.9 2.8 %collective-permute-start.6 = (bf16[272,256]{1,0:T(8,128)(2,1)S(1)}, bf16[272,256]{1,0:T(8,128)(2,1)S(1)}, u32[]{:S(2)}, u32[]{:S(2)}) collective-permute-start(bf16[272,256]{1,0:T(8,128)(2,1)S(1)} %get-tuple-element.13.refs_4_.refs_8_), channel_id=1, source_target_pairs={{0,20},{4,16},{8,28},{12,24},{16,4},{20,0},{24,12},{28,8},{1,21},{... | collective-permute-start | bytes 417800 | tf_op jit(solution)/shard_map/ppermute | solution.py:331
  15.7 2.3 %collective-permute-start.5 = (bf16[272,256]{1,0:T(8,128)(2,1)S(1)}, bf16[272,256]{1,0:T(8,128)(2,1)S(1)}, u32[]{:S(2)}, u32[]{:S(2)}) collective-permute-start(bf16[272,256]{1,0:T(8,128)(2,1)S(1)} %get-tuple-element.13.refs_4_.refs_8_), channel_id=1, source_target_pairs={{0,12},{4,8},{8,4},{12,0},{16,28},{20,24},{24,20},{28,16},{1,13},{... | collective-permute-start | bytes 417800 | tf_op jit(solution)/shard_map/ppermute | solution.py:331
  18.0 0.2 collective-permute-start.4
  18.2 1.0 %collective-permute-start.3 = (bf16[272,256]{1,0:T(8,128)(2,1)S(1)}, bf16[272,256]{1,0:T(8,128)(2,1)S(1)}, u32[]{:S(2)}, u32[]{:S(2)}) collective-permute-start(bf16[272,256]{1,0:T(8,128)(2,1)S(1)} %get-tuple-element.13.refs_4_.refs_8_), channel_id=1, source_target_pairs={{0,4},{4,0},{8,12},{12,8},{16,20},{20,16},{24,28},{28,24},{1,5},{5... | collective-permute-start | bytes 417800 | tf_op jit(solution)/shard_map/ppermute | solution.py:331
  19.2 1.8 %collective-permute-done.7.refs_9_.refs_13_ = bf16[272,256]{1,0:T(8,128)(2,1)S(1)} collective-permute-done((bf16[272,256]{1,0:T(8,128)(2,1)S(1)}, bf16[272,256]{1,0:T(8,128)(2,1)S(1)}, u32[]{:S(2)}, u32[]{:S(2)}) %collective-permute-start.7) | collective-permute-done | bytes 139296 | tf_op jit(solution)/shard_map/ppermute | solution.py:331
  21.0 9.8 %collective-permute-done.6.refs_8_.refs_12_ = bf16[272,256]{1,0:T(8,128)(2,1)S(1)} collective-permute-done((bf16[272,256]{1,0:T(8,128)(2,1)S(1)}, bf16[272,256]{1,0:T(8,128)(2,1)S(1)}, u32[]{:S(2)}, u32[]{:S(2)}) %collective-permute-start.6) | collective-permute-done | bytes 139296 | tf_op jit(solution)/shard_map/ppermute | solution.py:331
  30.8 2.9 %shard_map.87 = (f32[4,256]{1,0:T(4,128)S(1)}, f32[4,1792]{1,0:T(4,128)S(1)}, f32[7,1024]{1,0:T(8,128)S(1)}, f32[4,256]{1,0:T(4,128)S(1)}, f32[7,256]{1,0:T(8,128)S(1)}) custom-call(s32[3]{0:T(128)S(1)} %pad_add_fusion.here, bf16[272,256]{1,0:T(8,128)(2,1)S(1)} %get-tuple-element.12.refs_0_.refs_4_, ...), custom_call_target="tpu_custom_call" | custom-call | tf_op jit(solution)/shard_map/pallas_call | solution.py:350
  33.7 0.3 collective-permute-start.11
  34.0 1.2 %collective-permute-start.10 = (f32[4,256]{1,0:T(4,128)S(1)}, f32[4,256]{1,0:T(4,128)S(1)}, u32[]{:S(2)}, u32[]{:S(2)}) collective-permute-start(f32[4,256]{1,0:T(4,128)S(1)} %get-tuple-element.16.refs_0_), channel_id=1, source_target_pairs={{0,2},{1,3},{2,0},{3,1},{4,6},{5,7},{6,4},{7,5},{8,10},{9,11},{10,... | collective-permute-start | bytes 12296 | tf_op jit(solution)/shard_map/ppermute | solution.py:335
  35.2 0.4 collective-permute-start.9
  35.6 1.2 %collective-permute-done.11.refs_3_ = f32[4,256]{1,0:T(4,128)S(1)} collective-permute-done((f32[4,256]{1,0:T(4,128)S(1)}, f32[4,256]{1,0:T(4,128)S(1)}, u32[]{:S(2)}, u32[]{:S(2)}) %collective-permute-start.11) | collective-permute-done | bytes 4128 | tf_op jit(solution)/shard_map/ppermute | solution.py:335
  36.8 0.8 %collective-permute-done.10.refs_2_ = f32[4,256]{1,0:T(4,128)S(1)} collective-permute-done((f32[4,256]{1,0:T(4,128)S(1)}, f32[4,256]{1,0:T(4,128)S(1)}, u32[]{:S(2)}, u32[]{:S(2)}) %collective-permute-start.10) | collective-permute-done | bytes 4128 | tf_op jit(solution)/shard_map/ppermute | solution.py:335
  37.6 2.9 %shard_map.88 = f32[8,7,256]{2,1,0:T(8,128)S(1)} custom-call(s32[3]{0:T(128)S(1)} %pad_add_fusion.here, f32[4,256]{1,0:T(4,128)S(1)} %get-tuple-element.14.src_value, f32[7,1024]{1,0:T(8,128)S(1)} %get-tuple-element.15.col_bias, f32[4,256]{1,0:T(4,128)S(1)} %get-tuple-element.16.refs_0_, f32[4,256]{1,0:T(4,128)S(1)} %collective-permute-done.9.refs_1_, ...), custom_call_target="tpu_custom_call" | custom-call | tf_op jit(solution)/shard_map/pallas_call | solution.py:362
  40.6 12.3 %all_to_all.10.gathered = f32[8,7,256]{2,1,0:T(8,128)S(1)} all-to-all(f32[8,7,256]{2,1,0:T(8,128)S(1)} %shard_map.88), channel_id=1, replica_groups=mesh['pts'=8,'help'=4] {'pts'}, dimensions={0} | all-to-all | bytes 114688 | tf_op jit(solution)/shard_map/all_to_all | solution.py:368
  52.9 2.3 %shard_map.89.refs_0_ = f32[4,256]{1,0:T(4,128)S(1)} custom-call(f32[8,7,256]{2,1,0:T(8,128)S(1)} %all_to_all.10.gathered, f32[7,256]{1,0:T(8,128)S(1)} %get-tuple-element.17.dst_value, f32[4,1792]{1,0:T(4,128)S(1)} %get-tuple-element.18.row_bias, bf16[272,256]{1,0:T(8,128)(2,1)S(1)} %get-tuple-element.12.refs_0_.refs_4_, ...), custom_call_target="tpu_custom_call" | custom-call | tf_op jit(solution)/shard_map/pallas_call | solution.py:369
  55.2 0.1 collective-permute-start.14
  55.2 1.2 %collective-permute-start.13 = (f32[4,256]{1,0:T(4,128)S(1)}, f32[4,256]{1,0:T(4,128)S(1)}, u32[]{:S(2)}, u32[]{:S(2)}) collective-permute-start(f32[4,256]{1,0:T(4,128)S(1)} %shard_map.89.refs_0_), channel_id=1, source_target_pairs={{0,2},{1,3},{2,0},{3,1},{4,6},{5,7},{6,4},{7,5},{8,10},{9,11},{10,... | collective-permute-start | bytes 12296 | tf_op jit(solution)/shard_map/ppermute | solution.py:335
  56.5 0.6 collective-permute-start.12
  57.1 1.2 %collective-permute-done.14.refs_3_ = f32[4,256]{1,0:T(4,128)S(1)} collective-permute-done((f32[4,256]{1,0:T(4,128)S(1)}, f32[4,256]{1,0:T(4,128)S(1)}, u32[]{:S(2)}, u32[]{:S(2)}) %collective-permute-start.14) | collective-permute-done | bytes 4128 | tf_op jit(solution)/shard_map/ppermute | solution.py:335
  58.3 0.7 collective-permute-done.13.refs_2_
  58.9 3.4 %shard_map.90 = (f32[8,1,256]{2,1,0:T(1,128)S(1)}, f32[1,256]{1,0:T(1,128)}) custom-call(s32[3]{0:T(128)S(1)} %pad_add_fusion.here, f32[4,256]{1,0:T(4,128)S(1)} %get-tuple-element.14.src_value, f32[7,1024]{1,0:T(8,128)S(1)} %get-tuple-element.15.col_bias, f32[4,256]{1,0:T(4,128)S(1)} %shard_map.89.refs_0_, f32[4,256]{1,0:T(4,128)S(1)} %collective-permute-done.12.refs_1_, ...), custom_call_target="tpu_custom_call" | custom-call | tf_op jit(solution)/shard_map/pallas_call | solution.py:375
  62.3 8.9 %all_to_all.11.gathered = f32[8,1,256]{2,1,0:T(1,128)S(1)} all-to-all(f32[8,1,256]{2,1,0:T(1,128)S(1)} %get-tuple-element.21), channel_id=1, replica_groups=mesh['pts'=8,'help'=4] {'pts'}, dimensions={0} | all-to-all | bytes 16384 | tf_op jit(solution)/shard_map/all_to_all | solution.py:381
  71.2 0.6 shard_map.91
  (19 shorter events, 0.1 us)
Async XLA Ops:
  1.4 0.7 copy-start.3
  1.4 0.7 copy-start.4
  1.4 0.7 copy-start.2
  1.4 0.7 copy-start.5
  2.1 0.9 %copy-start = (bf16[256,256]{1,0:T(8,128)(2,1)S(1)}, bf16[256,256]{1,0:T(8,128)(2,1)}, u32[]{:S(2)}) copy-start(bf16[256,256]{1,0:T(8,128)(2,1)} %src.1) | copy-start | bytes 393220
  3.0 0.9 %copy-start.1 = (bf16[256,256]{1,0:T(8,128)(2,1)S(1)}, bf16[256,256]{1,0:T(8,128)(2,1)}, u32[]{:S(2)}) copy-start(bf16[256,256]{1,0:T(8,128)(2,1)} %dst.1) | copy-start | bytes 393220
  4.7 8.2 %collective-permute-start.2 = (bf16[272,256]{1,0:T(8,128)(2,1)S(1)}, bf16[272,256]{1,0:T(8,128)(2,1)S(1)}, u32[]{:S(2)}, u32[]{:S(2)}) collective-permute-start(bf16[272,256]{1,0:T(8,128)(2,1)S(1)} %get-tuple-element.12.refs_0_.refs_4_), channel_id=1, source_target_pairs={{0,3},{1,2},{2,1},{3,0},{4,7},{5,6},{6,5},{7,4},{8,11},{9,10},{10,... | collective-permute-start | bytes 417800 | tf_op jit(solution)/shard_map/ppermute | solution.py:335
  7.2 8.5 %collective-permute-start.1 = (bf16[272,256]{1,0:T(8,128)(2,1)S(1)}, bf16[272,256]{1,0:T(8,128)(2,1)S(1)}, u32[]{:S(2)}, u32[]{:S(2)}) collective-permute-start(bf16[272,256]{1,0:T(8,128)(2,1)S(1)} %get-tuple-element.12.refs_0_.refs_4_), channel_id=1, source_target_pairs={{0,2},{1,3},{2,0},{3,1},{4,6},{5,7},{6,4},{7,5},{8,10},{9,11},{10,... | collective-permute-start | bytes 417800 | tf_op jit(solution)/shard_map/ppermute | solution.py:335
  7.9 10.1 %collective-permute-start = (bf16[272,256]{1,0:T(8,128)(2,1)S(1)}, bf16[272,256]{1,0:T(8,128)(2,1)S(1)}, u32[]{:S(2)}, u32[]{:S(2)}) collective-permute-start(bf16[272,256]{1,0:T(8,128)(2,1)S(1)} %get-tuple-element.12.refs_0_.refs_4_), channel_id=1, source_target_pairs={{0,1},{1,0},{2,3},{3,2},{4,5},{5,4},{6,7},{7,6},{8,9},{9,8},{10,11... | collective-permute-start | bytes 417800 | tf_op jit(solution)/shard_map/ppermute | solution.py:335
  7.9 10.3 %collective-permute-start.8 = (bf16[272,256]{1,0:T(8,128)(2,1)S(1)}, bf16[272,256]{1,0:T(8,128)(2,1)S(1)}, u32[]{:S(2)}, u32[]{:S(2)}) collective-permute-start(bf16[272,256]{1,0:T(8,128)(2,1)S(1)} %get-tuple-element.13.refs_4_.refs_8_), channel_id=1, source_target_pairs={{0,28},{4,24},{8,20},{12,16},{16,12},{20,8},{24,4},{28,0},{1,29},{... | collective-permute-start | bytes 417800 | tf_op jit(solution)/shard_map/ppermute | solution.py:331
  12.7 8.3 %collective-permute-start.7 = (bf16[272,256]{1,0:T(8,128)(2,1)S(1)}, bf16[272,256]{1,0:T(8,128)(2,1)S(1)}, u32[]{:S(2)}, u32[]{:S(2)}) collective-permute-start(bf16[272,256]{1,0:T(8,128)(2,1)S(1)} %get-tuple-element.13.refs_4_.refs_8_), channel_id=1, source_target_pairs={{0,24},{4,28},{8,16},{12,20},{16,8},{20,12},{24,0},{28,4},{1,25},{... | collective-permute-start | bytes 417800 | tf_op jit(solution)/shard_map/ppermute | solution.py:331
  12.9 17.9 %collective-permute-start.6 = (bf16[272,256]{1,0:T(8,128)(2,1)S(1)}, bf16[272,256]{1,0:T(8,128)(2,1)S(1)}, u32[]{:S(2)}, u32[]{:S(2)}) collective-permute-start(bf16[272,256]{1,0:T(8,128)(2,1)S(1)} %get-tuple-element.13.refs_4_.refs_8_), channel_id=1, source_target_pairs={{0,20},{4,16},{8,28},{12,24},{16,4},{20,0},{24,12},{28,8},{1,21},{... | collective-permute-start | bytes 417800 | tf_op jit(solution)/shard_map/ppermute | solution.py:331
  15.7 15.1 %collective-permute-start.5 = (bf16[272,256]{1,0:T(8,128)(2,1)S(1)}, bf16[272,256]{1,0:T(8,128)(2,1)S(1)}, u32[]{:S(2)}, u32[]{:S(2)}) collective-permute-start(bf16[272,256]{1,0:T(8,128)(2,1)S(1)} %get-tuple-element.13.refs_4_.refs_8_), channel_id=1, source_target_pairs={{0,12},{4,8},{8,4},{12,0},{16,28},{20,24},{24,20},{28,16},{1,13},{... | collective-permute-start | bytes 417800 | tf_op jit(solution)/shard_map/ppermute | solution.py:331
  18.0 12.8 %collective-permute-start.4 = (bf16[272,256]{1,0:T(8,128)(2,1)S(1)}, bf16[272,256]{1,0:T(8,128)(2,1)S(1)}, u32[]{:S(2)}, u32[]{:S(2)}) collective-permute-start(bf16[272,256]{1,0:T(8,128)(2,1)S(1)} %get-tuple-element.13.refs_4_.refs_8_), channel_id=1, source_target_pairs={{0,8},{4,12},{8,0},{12,4},{16,24},{20,28},{24,16},{28,20},{1,9},{5... | collective-permute-start | bytes 417800 | tf_op jit(solution)/shard_map/ppermute | solution.py:331
  18.2 12.6 %collective-permute-start.3 = (bf16[272,256]{1,0:T(8,128)(2,1)S(1)}, bf16[272,256]{1,0:T(8,128)(2,1)S(1)}, u32[]{:S(2)}, u32[]{:S(2)}) collective-permute-start(bf16[272,256]{1,0:T(8,128)(2,1)S(1)} %get-tuple-element.13.refs_4_.refs_8_), channel_id=1, source_target_pairs={{0,4},{4,0},{8,12},{12,8},{16,20},{20,16},{24,28},{28,24},{1,5},{5... | collective-permute-start | bytes 417800 | tf_op jit(solution)/shard_map/ppermute | solution.py:331
  33.7 3.1 %collective-permute-start.11 = (f32[4,256]{1,0:T(4,128)S(1)}, f32[4,256]{1,0:T(4,128)S(1)}, u32[]{:S(2)}, u32[]{:S(2)}) collective-permute-start(f32[4,256]{1,0:T(4,128)S(1)} %get-tuple-element.16.refs_0_), channel_id=1, source_target_pairs={{0,3},{1,2},{2,1},{3,0},{4,7},{5,6},{6,5},{7,4},{8,11},{9,10},{10,... | collective-permute-start | bytes 12296 | tf_op jit(solution)/shard_map/ppermute | solution.py:335
  34.0 3.6 %collective-permute-start.10 = (f32[4,256]{1,0:T(4,128)S(1)}, f32[4,256]{1,0:T(4,128)S(1)}, u32[]{:S(2)}, u32[]{:S(2)}) collective-permute-start(f32[4,256]{1,0:T(4,128)S(1)} %get-tuple-element.16.refs_0_), channel_id=1, source_target_pairs={{0,2},{1,3},{2,0},{3,1},{4,6},{5,7},{6,4},{7,5},{8,10},{9,11},{10,... | collective-permute-start | bytes 12296 | tf_op jit(solution)/shard_map/ppermute | solution.py:335
  35.2 2.4 %collective-permute-start.9 = (f32[4,256]{1,0:T(4,128)S(1)}, f32[4,256]{1,0:T(4,128)S(1)}, u32[]{:S(2)}, u32[]{:S(2)}) collective-permute-start(f32[4,256]{1,0:T(4,128)S(1)} %get-tuple-element.16.refs_0_), channel_id=1, source_target_pairs={{0,1},{1,0},{2,3},{3,2},{4,5},{5,4},{6,7},{7,6},{8,9},{9,8},{10,11... | collective-permute-start | bytes 12296 | tf_op jit(solution)/shard_map/ppermute | solution.py:335
  55.2 3.1 %collective-permute-start.14 = (f32[4,256]{1,0:T(4,128)S(1)}, f32[4,256]{1,0:T(4,128)S(1)}, u32[]{:S(2)}, u32[]{:S(2)}) collective-permute-start(f32[4,256]{1,0:T(4,128)S(1)} %shard_map.89.refs_0_), channel_id=1, source_target_pairs={{0,3},{1,2},{2,1},{3,0},{4,7},{5,6},{6,5},{7,4},{8,11},{9,10},{10,... | collective-permute-start | bytes 12296 | tf_op jit(solution)/shard_map/ppermute | solution.py:335
  55.2 3.7 %collective-permute-start.13 = (f32[4,256]{1,0:T(4,128)S(1)}, f32[4,256]{1,0:T(4,128)S(1)}, u32[]{:S(2)}, u32[]{:S(2)}) collective-permute-start(f32[4,256]{1,0:T(4,128)S(1)} %shard_map.89.refs_0_), channel_id=1, source_target_pairs={{0,2},{1,3},{2,0},{3,1},{4,6},{5,7},{6,4},{7,5},{8,10},{9,11},{10,... | collective-permute-start | bytes 12296 | tf_op jit(solution)/shard_map/ppermute | solution.py:335
  56.5 2.4 %collective-permute-start.12 = (f32[4,256]{1,0:T(4,128)S(1)}, f32[4,256]{1,0:T(4,128)S(1)}, u32[]{:S(2)}, u32[]{:S(2)}) collective-permute-start(f32[4,256]{1,0:T(4,128)S(1)} %shard_map.89.refs_0_), channel_id=1, source_target_pairs={{0,1},{1,0},{2,3},{3,2},{4,5},{5,4},{6,7},{7,6},{8,9},{9,8},{10,11... | collective-permute-start | bytes 12296 | tf_op jit(solution)/shard_map/ppermute | solution.py:335
